TPU v7x, 128 devices: a whole 4x4x4 slice. The times are simulated.
128 devices in a mesh: order: 32 (over y, x, core), help: 4 (over z).
Axes of the slice: x: 4, y: 4, z: 4, core: 2. Of those that a mesh axis runs over, the one named last changes fastest.
Arguments:
- raw_feats: bfloat16 [128, 1024, 256], P(('order', 'help')), may hold values from -6 to 6
- serial: int32 [128, 1024], P(('order', 'help')), may hold values from 0 to 1023, each once within a row
- counts: int32 [128, 1], P(('order', 'help')), may hold values from 1 to 1024, as said below
- norm_gain: float32 [256], replicated, may hold values from 0.1 to 1.9
- w_qkv: bfloat16 [256, 768], replicated
- w_proj: bfloat16 [256, 256], replicated, may hold values from -0.375 to 0.375
- out_grad: bfloat16 [128, 1024, 256], P(('order', 'help')), may hold values from -6 to 6
- cluster: int32 [128, 1024], P(('order', 'help')), may hold values from 0 to 255, never falling along the last dimension, each value on 1 to 8 neighbouring positions
- joined: int32 [128], P(('order', 'help')), may hold values 0 or 1
Outputs:
- pooled: bfloat16 [128, 1024, 256], P(('order', 'help'))
- grad_feats: bfloat16 [128, 1024, 256], P(('order', 'help'))
- grad_qkv: float32 [256, 768], replicated
- grad_proj: float32 [256, 256], replicated
- grad_gain: float32 [256], replicated
Inputs may be any that keep to these rules, and one draw needn't show every extreme that they name: `serial`: each row is an ordering of the stored indices 0 to 1023. `counts`: the live points of a patch are its first ones. `cluster`: within a row, numbers start at 0, never fall, rise by at most one, and each number covers 1 to 8 points.
All inputs are finite; a program needn't handle non-finite values. No bound on the sum of `joined` on one device may be relied on, other than what follows from the above.
Results may differ from a plain program's by a relative error of at most 0.013.
The roundings to bfloat16 on the way count: a program that leaves them out, or rounds other values in their place, can miss the bound.
Values may be sent and summed in bfloat16 or wider, within the bound.
A program may use at most 192 MiB of HBM per device.

v0:
```python
import jax
import jax.numpy as jnp
from jax import lax
from jax.sharding import Mesh
from jax.sharding import PartitionSpec as P

H = 16
PATCH = 1024
GROUP = 8
ORDER = ("order_0", "order_1", "order_2")
ORDER_HELP = ("order_0", "order_1", "order_2", "help")


EPS = 1e-05
NEG = -1e30


def rows_for(lines, devices):
    spare = -lines.shape[0] % devices
    if not spare:
        return lines
    return jnp.concatenate([lines, jnp.zeros((spare, *lines.shape[1:]), lines.dtype)])


def sent_to_all(array, axis):
    copies = jnp.broadcast_to(array, (lax.axis_size(axis), *array.shape))
    return lax.all_to_all(copies, axis, split_axis=0, concat_axis=0, tiled=True)


def in_order(pieces, dim):
    lengths = list(pieces.shape[1:])
    lengths[dim] *= pieces.shape[0]
    return jnp.moveaxis(pieces, 0, dim).reshape(lengths)


def whole_of(array, axes, dim):
    far, near = axes
    initial = sent_to_all(array, far)
    pieces = jnp.swapaxes(sent_to_all(initial, near), 0, 1)
    return in_order(pieces.reshape(-1, *array.shape), dim)


def split_up(array, dim, devices):
    before, after = (array.shape[:dim], array.shape[dim + 1 :])
    return jnp.moveaxis(array.reshape(*before, devices, -1, *after), dim, 0)


def sent_and_summed(array, axis, dim):
    devices = lax.axis_size(axis)
    pieces = lax.all_to_all(split_up(array, dim, devices), axis, 0, 0, tiled=True)
    return jnp.sum(pieces, axis=0)


def sum_in_two_steps(array, axes, dim):
    far, near = axes
    own = sent_and_summed(split_up(array, dim, lax.axis_size(far)), near, dim + 1)
    return jnp.sum(lax.all_to_all(own, far, 0, 0, tiled=True), axis=0)


def sum_by_parts(array, axes):
    padded = rows_for(array, lax.axis_size(axes[0]) * lax.axis_size(axes[1]))
    whole = whole_of(sum_in_two_steps(padded, axes, 0), axes, 0)
    return lax.slice_in_dim(whole, 0, len(array)).reshape(array.shape)


def together(arrays, axis):
    line, at, outs = (jnp.concatenate([a.reshape(-1) for a in arrays]), 0, [])
    total = sum_by_parts(line, axis)
    for a in arrays:
        outs.append(total[at : at + a.size].reshape(a.shape))
        at += a.size
    return tuple(outs)


def extended(array, sides, width):
    edges = {}
    for axis, dim in sides:
        devices, length = (lax.axis_size(axis), array.shape[dim])
        up = [(i, (i + 1) % devices) for i in range(devices - 1)]
        last = lax.slice_in_dim(array, length - width, length, axis=dim)
        initial = lax.slice_in_dim(array, 0, width, axis=dim)
        edges[dim] = (
            lax.ppermute(last, axis, up),
            lax.ppermute(initial, axis, [(b, a) for a, b in up]),
        )
    done = []
    for _, dim in sides:
        low, high = edges[dim]
        around = [(width, width) if d in done else (0, 0) for d in range(array.ndim)]
        array = jnp.concatenate([jnp.pad(low, around), array, jnp.pad(high, around)], axis=dim)
        done.append(dim)
    return array


def head_block(queries, key_rows, value_rows, alive_mask):
    score_scale = queries.shape[-1] ** (-0.5)
    scores = (
        jnp.einsum("qhd,khd->hqk", queries, key_rows, preferred_element_type=jnp.float32)
        * score_scale
    )
    scores = jnp.where(alive_mask[None, None, :], scores, NEG)
    row_peak = jnp.max(scores, axis=-1, keepdims=True)
    exp_terms = jnp.exp(scores - row_peak)
    weights = (exp_terms / jnp.sum(exp_terms, axis=-1, keepdims=True)).astype(jnp.bfloat16)
    mixed_out = jnp.einsum("hqk,khd->qhd", weights, value_rows, preferred_element_type=jnp.float32)
    return jnp.where(alive_mask[:, None, None], mixed_out, 0.0).astype(jnp.bfloat16)


def attend_patch(qkv_in, count_in, head_size):
    checked_block = jax.checkpoint(head_block)
    row_total = qkv_in.shape[0]
    chan_width = qkv_in.shape[2]
    heads_here = chan_width // head_size
    group_heads = min(4, heads_here)
    alive_mask = jnp.arange(row_total, dtype=jnp.int32) < count_in
    blocks = qkv_in.reshape(
        row_total, 3, heads_here // group_heads, group_heads, head_size
    ).transpose(2, 0, 1, 3, 4)

    def one_block(head_group):
        return checked_block(head_group[:, 0], head_group[:, 1], head_group[:, 2], alive_mask)

    mixed_out = lax.map(one_block, blocks)
    return mixed_out.transpose(1, 0, 2, 3).reshape(row_total, chan_width)


def attend_split(qkv_in, count_in, head_size):
    half_rows = qkv_in.shape[0] // 2

    def short_patch(operands):
        half_out = attend_patch(operands[0][:half_rows], operands[1], head_size)
        return jnp.concatenate([half_out, jnp.zeros_like(half_out)], axis=0)

    def whole_patch(operands):
        return attend_patch(operands[0], operands[1], head_size)

    return lax.cond(count_in <= half_rows, short_patch, whole_patch, (qkv_in, count_in))


def attend_all(qkv_in, patch_counts, head_size):

    def per_patch(operands):
        return attend_split(operands[0], operands[1], head_size)

    return lax.map(per_patch, (qkv_in, patch_counts))


def layer_stats(rows_in):
    values = rows_in.astype(jnp.float32)
    centred = values - jnp.mean(values, axis=-1, keepdims=True)
    inv_std = lax.rsqrt(jnp.mean(centred * centred, axis=-1, keepdims=True) + EPS)
    return (centred * inv_std, inv_std)


def norm_backward(grad_norm, normed, inv_std):
    mean_grad = jnp.mean(grad_norm, axis=-1, keepdims=True)
    mean_cross = jnp.mean(grad_norm * normed, axis=-1, keepdims=True)
    return inv_std * (grad_norm - mean_grad - normed * mean_cross)


def window_max(block_out, group_ids):
    row_total, chan_width = block_out.shape
    reach_rows = GROUP - 1
    pad_vals = jnp.full((reach_rows, chan_width), -jnp.inf, block_out.dtype)
    pad_ids = jnp.full((reach_rows,), -1, jnp.int32)
    padded_vals = jnp.concatenate([pad_vals, block_out, pad_vals], axis=0)
    padded_ids = jnp.concatenate([pad_ids, group_ids, pad_ids], axis=0)
    group_max = block_out
    for offset in range(-reach_rows, reach_rows + 1):
        window_vals = padded_vals[reach_rows + offset : reach_rows + offset + row_total]
        same_group = padded_ids[reach_rows + offset : reach_rows + offset + row_total] == group_ids
        group_max = jnp.maximum(group_max, jnp.where(same_group[:, None], window_vals, -jnp.inf))
    return group_max


def body(raw_feats, serial, counts, norm_gain, w_qkv, w_proj, out_grad, cluster, joined):
    raw_rows = raw_feats[0]
    row_total, chan_width = raw_rows.shape
    head_size = chan_width // H
    patch_total = row_total // PATCH
    shard_total = lax.axis_size(ORDER) * lax.axis_size("help")
    point_scale = 2.0 * row_total ** (-0.5)
    order_index = serial[0]
    gathered = jnp.take(raw_rows, order_index, axis=0)
    normed, inv_std = layer_stats(gathered)
    hidden = (normed * norm_gain).astype(jnp.bfloat16)
    packed = jnp.dot(hidden, w_qkv, preferred_element_type=jnp.float32).astype(jnp.bfloat16)
    packed = packed.reshape(patch_total, PATCH, 3, chan_width)
    grad_out = out_grad[0]
    back_proj = jnp.einsum(
        "nd,cd->nc", grad_out, w_proj, preferred_element_type=jnp.float32
    ).astype(jnp.bfloat16)

    def attend_own(qkv_in):
        return attend_all(qkv_in, counts[0], head_size)

    own_out, pullback = jax.vjp(attend_own, packed)
    grad_packed = pullback(back_proj.reshape(patch_total, PATCH, chan_width))[0]
    attended = own_out.reshape(row_total, chan_width)
    block_out = (
        gathered.astype(jnp.float32) + jnp.dot(attended, w_proj, preferred_element_type=jnp.float32)
    ).astype(jnp.bfloat16)
    grad_flat = grad_packed.reshape(row_total, 3 * chan_width)
    grad_hidden = jnp.einsum("nk,ck->nc", grad_flat, w_qkv, preferred_element_type=jnp.float32)
    qkv_part = (
        jnp.einsum("nc,nk->ck", hidden, grad_flat, preferred_element_type=jnp.float32) * point_scale
    )
    proj_part = (
        jnp.einsum("nc,nd->cd", attended, grad_out, preferred_element_type=jnp.float32)
        * point_scale
    )
    gain_part = jnp.sum(grad_hidden * normed, axis=0) * point_scale
    grad_qkv, grad_proj, grad_gain = together(
        (qkv_part, proj_part, gain_part), (("order_0", "order_1"), ("order_2", "help"))
    )
    group_ids = cluster[0]
    group_max = window_max(block_out, group_ids)
    position = lax.axis_index(ORDER_HELP)
    linked = joined[0] > 0
    head_edge = jnp.where(linked, group_max[0], -jnp.inf)
    edge_rows = jnp.stack([head_edge, group_max[-1]], axis=0)
    rim_rows = extended(edge_rows, ((ORDER_HELP, 0),), 1)
    from_prev = rim_rows[0]
    from_next = rim_rows[3]
    first_mask = (group_ids == group_ids[0]) & linked & (position > 0)
    last_mask = (group_ids == group_ids[-1]) & (position < shard_total - 1)
    group_max = jnp.where(
        first_mask[:, None], jnp.maximum(group_max, from_prev[None, :]), group_max
    )
    group_max = jnp.where(last_mask[:, None], jnp.maximum(group_max, from_next[None, :]), group_max)
    grad_input = (
        grad_out.astype(jnp.float32) + norm_backward(grad_hidden * norm_gain, normed, inv_std)
    ).astype(jnp.bfloat16)
    inverse = (
        jnp.zeros((row_total,), jnp.int32)
        .at[order_index]
        .set(jnp.arange(row_total, dtype=jnp.int32))
    )
    grad_feats = jnp.take(grad_input, inverse, axis=0)
    return (group_max[None], grad_feats[None], grad_qkv, grad_proj, grad_gain)


def solution(mesh):
    torus = Mesh(
        mesh.devices.reshape(4, 4, 2, mesh.shape["help"]), ("order_0", "order_1", "order_2", "help")
    )
    placed = (
        P(ORDER_HELP, None, None),
        P(ORDER_HELP, None),
        P(ORDER_HELP, None),
        P(),
        P(),
        P(),
        P(ORDER_HELP, None, None),
        P(ORDER_HELP, None),
        P(ORDER_HELP),
    )
    return jax.shard_map(
        body,
        mesh=torus,
        in_specs=placed,
        out_specs=(P(ORDER_HELP, None, None), P(ORDER_HELP, None, None), P(), P(), P()),
        check_vma=False,
    )
```

profile of v0, /device:TPU:1, one launch (start us, length us, event | category | flops | bytes accessed | tf_op | source)
XLA Modules:
  0.0 457.6 jit_solution(14003048205626105550)
XLA Ops:
  2.1 3.9 gather_fusion
  9.3 46.1 %conditional.2 = (bf16[1024,256]{0,1:T(8,128)(2,1)}, pred[1024]{0:T(1024)(128)(4,1)S(1)}, bf16[4,1024,4,16]{3,2,1,0:T(4,128)(2,1)}, bf16[4,1024,4,16]{3,2,1,0:T(...) conditional(s32[]{:T(128)} %convert_element_type.227, ...), branch_computations={%region_2.8_spmd, %region_7.0_spmd} | conditional | flops 293734400 | bytes 43815720 | solution.py:137
  11.9 33.5 %while.80 = (s32[]{:T(128)}, bf16[4,512,4,16]{1,3,2,0:T(8,128)(2,1)S(1)}, bf16[4,512,4,16]{1,3,2,0:T(8,128)(2,1)}, bf16[4,512,4,16]{1,3,2,0:T(8,128)(2,1)}, bf16...) while((s32[]{:T(128)}, ...), condition=%wide.region_11.12_spmd.clone.clone, body=%wide.region_8.11_spmd.clone.clone.sunk | while | flops 73466368 | bytes 9455197 | solution.py:123
  12.8 4.2 fusion.306
  21.2 4.2 fusion.306
  29.6 4.2 fusion.306
  38.0 4.2 fusion.306
  56.1 75.2 %conditional.3 = (bf16[1024,768]{0,1:T(8,128)(2,1)}) conditional(s32[]{:T(128)} %convert_element_type.227, (bf16[1024,256]{1,0:T(8,128)(2,1)S(1)}, bf16[4,1024,4,16]{3,2,1,0:T(4,128)(2,1)}, bf16[4,1024,4,16]{3,2,1,0:T(4,128)(2,1)}, bf16[4,1024,4,16]{3,2,1,0:T(4,128)(2,1)}, pred[1024]{0:T(1024)(128)(4,1)}) %tuple.261, ...), branch_computations={%region_12.21_spmd, %region_20.29_spmd} | conditional | flops 836304896 | bytes 190164480 | solution.py:137
  64.7 65.2 %while.82 = (s32[]{:T(128)}, bf16[4,512,3,4,16]{1,4,3,0,2:T(8,128)(2,1)S(1)}, bf16[4,512,4,16]{1,3,2,0:T(8,128)(2,1)}, bf16[4,512,4,16]{1,3,2,0:T(8,128)(2,1)}, ...) while((s32[]{:T(128)}, ...), condition=%wide.region_27.28_spmd, body=%wide.region_21.27_spmd.sunk | while | flops 209485824 | bytes 42651252 | solution.py:123
  71.6 3.5 convert_reduce_fusion.5
  87.9 3.5 convert_reduce_fusion.5
  104.3 3.5 convert_reduce_fusion.5
  120.6 3.5 convert_reduce_fusion.5
  133.8 3.8 fusion.166
  143.5 239.4 %all-to-all-start = ((f32[8,16,2050]{2,1,0:T(8,128)}), f32[8,16,2050]{2,1,0:T(8,128)S(1)}, u32[]{:S(2)}, u32[]{:S(2)}) async-start(f32[8,16,2050]{2,1,0:T(8,128)} %copy.101), calls=%async_computation | async-start | bytes 2228224 | tf_op jit(solution)/shard_map/all_to_all | solution.py:50
  392.0 3.6 collective-permute-start.1
  395.7 4.3 scatter_custom_fusion
  403.1 6.5 %all-to-all-start.1 = ((f32[16,1,2050]{2,1,0:T(1,128)}), f32[16,1,2050]{2,1,0:T(1,128)S(1)}, u32[]{:S(2)}, u32[]{:S(2)}) async-start(f32[16,1,2050]{2,1,0:T(1,128)} %all_to_all.19), calls=%async_computation.1 | async-start | bytes 278528 | tf_op jit(solution)/shard_map/all_to_all | solution.py:57
  409.6 3.9 gather_fusion.1
  417.3 3.7 all-to-all-start.2
  421.0 6.9 %all-to-all-done.2 = f32[16,1,2050]{2,1,0:T(1,128)S(1)} async-done(((f32[16,1,2050]{2,1,0:T(1,128)}), f32[16,1,2050]{2,1,0:T(1,128)S(1)}, u32[]{:S(2)}, u32[]{:S(2)}) %all-to-all-start.2) | async-done | bytes 131232 | tf_op jit(solution)/shard_map/all_to_all | solution.py:27
  429.1 6.8 %all-to-all-start.3 = ((f32[8,16,2050]{2,1,0:T(8,128)}), f32[8,16,2050]{2,1,0:T(8,128)S(1)}, u32[]{:S(2)}, u32[]{:S(2)}) async-start(f32[8,16,2050]{2,1,0:T(8,128)} %broadcast_in_dim.537), calls=%async_computation.3 | async-start | bytes 2228224 | tf_op jit(solution)/shard_map/all_to_all | solution.py:27
  437.6 4.7 %fusion.168 = bf16[1,1024,256]{2,1,0:T(8,128)(2,1)} fusion(pred[1024]{0:T(1024)(128)(4,1)S(1)} %and_and_fusion, pred[1024]{0:T(1024)(128)(4,1)S(1)} %get-tuple-element.891, bf16[256]{0:T(256)(128)(2,1)S(1)} %reduce.2, bf16[256]{0:T(256)(128)(2,1)S(1)} %reduce.1, pred[1024]{0:T(1024)(128)(4,1)S(1)} %get-tuple-element.905, ...), kind=kLoop, calls=%fused_computation.204 | loop fusion | flops 14155776 | bytes 1065984 | tf_op jit(solution)/shard_map/broadcast_in_dim | solution.py:240
  442.3 9.2 %all-to-all-done.3 = f32[8,16,2050]{2,1,0:T(8,128)S(1)} async-done(((f32[8,16,2050]{2,1,0:T(8,128)}), f32[8,16,2050]{2,1,0:T(8,128)S(1)}, u32[]{:S(2)}, u32[]{:S(2)}) %all-to-all-start.3) | async-done | bytes 1049632 | tf_op jit(solution)/shard_map/all_to_all | solution.py:27
  (170 shorter events, 118.6 us)
Async XLA Ops:
  0.6 7.0 %copy-start.32 = (f32[256]{0:T(256)S(1)}, f32[256]{0:T(256)}, u32[]{:S(2)}) copy-start(f32[256]{0:T(256)} %param.26) | copy-start | bytes 3076
  0.7 7.0 %copy-start.34 = (bf16[256,768]{1,0:T(8,128)(2,1)S(1)}, bf16[256,768]{1,0:T(8,128)(2,1)}, u32[]{:S(2)}) copy-start(bf16[256,768]{1,0:T(8,128)(2,1)} %param.27) | copy-start | bytes 1179652
  2.1 7.1 %copy-start.28 = (pred[1024]{0:T(1024)(128)(4,1)}, pred[1024]{0:T(1024)(128)(4,1)S(1)}, u32[]{:S(2)}) copy-start(pred[1024]{0:T(1024)(128)(4,1)S(1)} %compare_and_fusion.1) | copy-start | bytes 3076
  9.3 46.2 %copy-start.4 = (bf16[1,1024,256]{2,1,0:T(8,128)(2,1)S(1)}, bf16[1,1024,256]{2,1,0:T(8,128)(2,1)}, u32[]{:S(2)}) copy-start(bf16[1,1024,256]{2,1,0:T(8,128)(2,1)} %param.29) | copy-start | bytes 1572868
  9.3 46.2 %copy-start.22 = (bf16[256,256]{1,0:T(8,128)(2,1)S(1)}, bf16[256,256]{1,0:T(8,128)(2,1)}, u32[]{:S(2)}) copy-start(bf16[256,256]{1,0:T(8,128)(2,1)} %param.28) | copy-start | bytes 393220
  56.1 75.2 %copy-start.3 = (bf16[1024,256]{1,0:T(8,128)(2,1)S(1)}, bf16[1024,256]{1,0:T(8,128)(2,1)}, u32[]{:S(2)}) copy-start(bf16[1024,256]{1,0:T(8,128)(2,1)} %copy-done.2) | copy-start | bytes 1572868
  56.1 75.2 %copy-start.25 = (f32[1024]{0:T(1024)S(1)}, f32[1024]{0:T(1024)}, u32[]{:S(2)}) copy-start(f32[1024]{0:T(1024)} %copy-done.24) | copy-start | bytes 12292
  56.1 75.2 %copy-start.29 = (pred[1024]{0:T(1024)(128)(4,1)S(1)}, pred[1024]{0:T(1024)(128)(4,1)}, u32[]{:S(2)}) copy-start(pred[1024]{0:T(1024)(128)(4,1)} %copy-done.28) | copy-start | bytes 3076
  133.8 3.8 copy-start.5
  139.2 243.8 %copy-start.19 = (bf16[1024,256]{0,1:T(8,128)(2,1)S(1)}, bf16[1024,256]{0,1:T(8,128)(2,1)}, u32[]{:S(2)}) copy-start(bf16[1024,256]{0,1:T(8,128)(2,1)} %get-tuple-element.585) | copy-start | bytes 1572868
  139.2 243.7 %copy-start.23 = (bf16[256,256]{1,0:T(8,128)(2,1)S(1)}, bf16[256,256]{1,0:T(8,128)(2,1)}, u32[]{:S(2)}) copy-start(bf16[256,256]{1,0:T(8,128)(2,1)} %param.28) | copy-start | bytes 393220
  140.2 243.1 %copy-start.27 = (s32[1,1024]{1,0:T(1,128)S(1)}, s32[1,1024]{1,0:T(1,128)}, u32[]{:S(2)}) copy-start(s32[1,1024]{1,0:T(1,128)} %param.30) | copy-start | bytes 12292
  142.2 253.4 %copy-start.26 = (s32[1,1024]{1,0:T(1,128)S(1)}, s32[1,1024]{1,0:T(1,128)}, u32[]{:S(2)}) copy-start(s32[1,1024]{1,0:T(1,128)} %param.24) | copy-start | bytes 12292
  142.3 257.8 %copy-start.31 = (f32[1024]{0:T(1024)S(1)}, f32[1024]{0:T(1024)}, u32[]{:S(2)}) copy-start(f32[1024]{0:T(1024)} %copy-done.30) | copy-start | bytes 12292
  142.3 257.8 %copy-start.33 = (f32[256]{0:T(256)S(1)}, f32[256]{0:T(256)}, u32[]{:S(2)}) copy-start(f32[256]{0:T(256)} %param.26) | copy-start | bytes 3076
  143.5 258.7 %all-to-all-start = ((f32[8,16,2050]{2,1,0:T(8,128)}), f32[8,16,2050]{2,1,0:T(8,128)S(1)}, u32[]{:S(2)}, u32[]{:S(2)}) async-start(f32[8,16,2050]{2,1,0:T(8,128)} %copy.101), calls=%async_computation | async-start | bytes 2228224 | tf_op jit(solution)/shard_map/all_to_all | solution.py:50
  383.3 16.7 %copy-start.15 = (bf16[1024,256]{1,0:T(8,128)(2,1)}, bf16[1024,256]{1,0:T(8,128)(2,1)S(1)}, u32[]{:S(2)}) copy-start(bf16[1024,256]{1,0:T(8,128)(2,1)S(1)} %fusion.152) | copy-start | bytes 1572868
  388.7 48.8 %collective-permute-start = (bf16[1,256]{1,0:T(2,128)(2,1)S(1)}, bf16[1,256]{1,0:T(2,128)(2,1)S(1)}, u32[]{:S(2)}, u32[]{:S(2)}) collective-permute-start(bf16[1,256]{1,0:T(2,128)(2,1)S(1)} %get-tuple-element.889), channel_id=1, source_target_pairs={{0,1},{1,2},{2,3},{3,4},{4,5},{5,6},{6,7},{7,8},{8,9},{9,10},{10,1... | collective-permute-start | bytes 1544 | tf_op jit(solution)/shard_map/ppermute | solution.py:83
  392.0 45.6 %collective-permute-start.1 = (bf16[1,256]{1,0:T(2,128)(2,1)S(1)}, bf16[1,256]{1,0:T(2,128)(2,1)S(1)}, u32[]{:S(2)}, u32[]{:S(2)}) collective-permute-start(bf16[1,256]{1,0:T(2,128)(2,1)S(1)} %get-tuple-element.890), channel_id=1, source_target_pairs={{1,0},{2,1},{3,2},{4,3},{5,4},{6,5},{7,6},{8,7},{9,8},{10,9},{11,1... | collective-permute-start | bytes 1544 | tf_op jit(solution)/shard_map/ppermute | solution.py:84
  403.1 13.4 %all-to-all-start.1 = ((f32[16,1,2050]{2,1,0:T(1,128)}), f32[16,1,2050]{2,1,0:T(1,128)S(1)}, u32[]{:S(2)}, u32[]{:S(2)}) async-start(f32[16,1,2050]{2,1,0:T(1,128)} %all_to_all.19), calls=%async_computation.1 | async-start | bytes 278528 | tf_op jit(solution)/shard_map/all_to_all | solution.py:57
  409.6 28.0 %copy-start.16 = (bf16[1024,256]{1,0:T(8,128)(2,1)S(1)}, bf16[1024,256]{1,0:T(8,128)(2,1)}, u32[]{:S(2)}) copy-start(bf16[1024,256]{1,0:T(8,128)(2,1)} %copy-done.15) | copy-start | bytes 1572868
  417.3 10.7 %all-to-all-start.2 = ((f32[16,1,2050]{2,1,0:T(1,128)}), f32[16,1,2050]{2,1,0:T(1,128)S(1)}, u32[]{:S(2)}, u32[]{:S(2)}) async-start(f32[16,1,2050]{2,1,0:T(1,128)} %broadcast_in_dim.536), calls=%async_computation.2 | async-start | bytes 278528 | tf_op jit(solution)/shard_map/all_to_all | solution.py:27
  429.1 22.5 %all-to-all-start.3 = ((f32[8,16,2050]{2,1,0:T(8,128)}), f32[8,16,2050]{2,1,0:T(8,128)S(1)}, u32[]{:S(2)}, u32[]{:S(2)}) async-start(f32[8,16,2050]{2,1,0:T(8,128)} %broadcast_in_dim.537), calls=%async_computation.3 | async-start | bytes 2228224 | tf_op jit(solution)/shard_map/all_to_all | solution.py:27
  451.6 6.0 %copy-start.1 = (bf16[1,1024,256]{2,1,0:T(8,128)(2,1)S(1)}, bf16[1,1024,256]{2,1,0:T(8,128)(2,1)}, u32[]{:S(2)}) copy-start(bf16[1,1024,256]{2,1,0:T(8,128)(2,1)} %param.23) | copy-start | bytes 1572868
  (5 other events, 10.5 us)
where the time goes:
time: 458 us
  starting transfers between devices  263 us (57%)
  matrix products  79.2 us (17%)
  local copies, waits for them, and re-layouts  51.2 us (11%)
  other arithmetic  33.1 us (7%)
  waiting for transfers between devices  19.2 us (4%)
  loops' own time  9.04 us (2%)
    all_to_all x1, starting transfers between devices, sent_and_summed(): lax.all_to_all(split_up(array, dim, devices), axis, 0, 0, tiled=True)  239 us
    dot_general x12, matrix products, head_block(): jnp.einsum('hqk,khd->qhd', weights, value_rows, preferred_element_type=jn...  31.8 us
    dot_general x12, matrix products, head_block(): jnp.einsum('qhd,khd->hqk', queries, key_rows, preferred_element_type=jnp....  20.8 us
    sub x4, matrix products, head_block(): exp_terms = jnp.exp(scores - row_peak)  16.8 us
    all_to_all x2, waiting for transfers between devices, sent_to_all(): return lax.all_to_all(copies, axis, split_axis=0, concat_axis=0, tiled=True)  16.2 us
    squeeze x12, local copies, waits for them, and re-layouts, attend_patch(): mixed_out = lax.map(one_block, blocks)  10.7 us
    all_to_all x2, starting transfers between devices, sent_to_all(): return lax.all_to_all(copies, axis, split_axis=0, concat_axis=0, tiled=True)  10.5 us
    another operation x6, local copies, waits for them, and re-layouts  9.47 us
  transfers between devices with their start and end apart: 6, of which 3 were waited for; matrix products, arithmetic and copies ran while one was open for 5% of the time, Pallas kernels for 0%

commit v1 on v0

v1 whole, which is shorter than its diff:
```python
import math

import jax
import jax.numpy as jnp
from jax import lax
from jax.experimental import pallas as pl
from jax.experimental.pallas import tpu as pltpu
from jax.sharding import Mesh
from jax.sharding import PartitionSpec as P

H = 16
C = 256
N = 1024
HD = 16
QB = 256
NQ = N // QB
GROUP = 8
ORDER_HELP = ("order_0", "order_1", "order_2", "help")
EPS = 1e-05
NEG = -1e30
SCALE = HD**-0.5
QSCALE = SCALE * math.log2(math.e)
POINT_SCALE = 2.0 * N**-0.5
F32 = jnp.float32
BF16 = jnp.bfloat16
MESH = pl.DeviceIdType.MESH
VMEM = pltpu.VMEM


def iota(shape, dim):
    return lax.broadcasted_iota(jnp.int32, shape, dim)


def mm(a, b):
    return jnp.dot(a, b, preferred_element_type=F32)


def mm_nt(a, b):
    return lax.dot_general(a, b, (((1,), (1,)), ((), ())), preferred_element_type=F32)


def split3(x):
    hi = x.astype(BF16)
    rest = x - hi.astype(F32)
    mid = rest.astype(BF16)
    lo = (rest - mid.astype(F32)).astype(BF16)
    return hi, mid, lo


def local_kernel(
    raw_ref,
    serial_ref,
    counts_ref,
    gain_ref,
    wqkv_ref,
    wproj_ref,
    og_ref,
    cluster_ref,
    pooled_ref,
    gfeats_ref,
    send_ref,
    gsum_ref,
    edge_ref,
    gath_ref,
    hid_ref,
    normed_ref,
    inv_ref,
    pT_ref,
    doT_ref,
    ka_ref,
    va_ref,
    qa_ref,
    vt_ref,
    e_ref,
    ds_ref,
    attT_ref,
    gpT_ref,
    dk_ref,
    dv_ref,
    grad_ref,
    dx_ref,
    bo_ref,
):
    n_live = counts_ref[0, 0]
    gain = gain_ref[...]
    serial_row = serial_ref[...]
    serial_cols = jnp.transpose(jnp.broadcast_to(serial_row.astype(F32), (128, N)))
    lane128 = iota((QB, 128), 1).astype(F32)

    for t in range(4):
        rows = pl.ds(t * QB, QB)
        sc = serial_cols[t * QB : (t + 1) * QB]
        onehot = jnp.concatenate(
            [jnp.where(sc == lane128 + float(128 * b), 1.0, 0.0).astype(BF16) for b in range(8)],
            axis=1,
        )
        x = mm(onehot, raw_ref[...])
        gath_ref[rows, :] = x.astype(BF16)
        centred = x - jnp.mean(x, axis=1, keepdims=True)
        inv = lax.rsqrt(jnp.mean(centred * centred, axis=1, keepdims=True) + EPS)
        normed = centred * inv
        normed_ref[rows, :] = normed
        inv_ref[rows, :] = inv
        hid = (normed * gain).astype(BF16)
        hid_ref[rows, :] = hid
        packed = mm(hid, wqkv_ref[...]).astype(BF16)
        pT_ref[:, rows] = jnp.transpose(packed)
        bp = mm_nt(og_ref[rows, :], wproj_ref[...]).astype(BF16)
        bpT = jnp.transpose(bp)
        lane = iota((C, QB), 1) + t * QB
        doT_ref[:, rows] = jnp.where(lane < n_live, bpT.astype(F32), 0.0).astype(BF16)
        key_live = (iota((QB, C), 0) + t * QB) < n_live
        kcols = packed[:, C : 2 * C]
        vcols = packed[:, 2 * C :]
        for b in range(4):
            cols = pl.ds(b * C, C)
            chan = iota((C, C), 0)
            place = iota((C, C), 1)
            spot = place % 64
            same = ((place // 64 + 4 * b) == chan // HD) & (spot % HD == chan % HD)
            rep_k = jnp.where(same & (spot < 3 * HD), 1.0, 0.0).astype(BF16)
            rep_v = jnp.where(same & (spot < 2 * HD), 1.0, 0.0).astype(BF16)
            spot_r = iota((QB, C), 1) % 64
            ka = mm(kcols, rep_k)
            ka = jnp.where((spot_r >= 48) & (spot_r < 51), 1.0, ka)
            ka = jnp.where((spot_r == 51) & jnp.logical_not(key_live), NEG, ka)
            ka_ref[rows, cols] = ka.astype(BF16)
            va = mm(vcols, rep_v)
            va = jnp.where((spot_r >= 32) & (spot_r < 35), 1.0, va)
            va_ref[rows, cols] = va.astype(BF16)

    def prep(h, carry):
        q = pT_ref[pl.ds(h * HD, HD), :].astype(F32)
        k = pT_ref[pl.ds(C + h * HD, HD), :].astype(F32)
        v = pT_ref[pl.ds(2 * C + h * HD, HD), :]
        do = doT_ref[pl.ds(h * HD, HD), :]
        q = q * QSCALE
        hi, mid, lo = split3(q)
        row = iota((HD, N), 0)
        tail = jnp.where(row == 3, 1.0, 0.0).astype(BF16)
        zeros = jnp.zeros((64, N), BF16)
        base = pl.multiple_of(h * 128, 128)
        half = pl.multiple_of((h % 2) * 64, 64)
        qa_ref[pl.ds(pl.multiple_of(base + half, 64), 64), :] = jnp.concatenate(
            [hi, mid, lo, tail], axis=0
        )
        qa_ref[pl.ds(pl.multiple_of(base + 64 - half, 64), 64), :] = zeros
        ones = jnp.where(row == 0, 1.0, 0.0).astype(BF16)
        vt_ref[pl.ds(h * 32, 32), :] = jnp.concatenate([v, ones], axis=0)
        q2 = jnp.max(jnp.sum(q * q, axis=0, keepdims=True))
        k2 = jnp.max(jnp.sum(k * k, axis=0, keepdims=True))
        vmax = jnp.max(jnp.abs(v.astype(F32)))
        dmax = jnp.max(jnp.abs(do.astype(F32)))
        tame = (q2 * k2 <= 8100.0) & (vmax <= 4096.0) & (dmax <= 4096.0)

        @pl.when(jnp.logical_not(tame))
        def _():
            lanes = pl.ds(pl.multiple_of((h // 2) * 128, 128), 128)
            for t in range(NQ):
                cols = pl.ds(t * QB, QB)
                peak = jnp.full((1, QB), -jnp.inf, F32)
                for r in range(4):
                    s = mm(ka_ref[pl.ds(r * QB, QB), lanes], qa_ref[pl.ds(base, 128), cols])
                    peak = jnp.maximum(peak, jnp.max(s, axis=0, keepdims=True))
                p_hi, p_mid, p_lo = split3(-peak)
                rowq = iota((HD, QB), 0)
                shift = jnp.where(rowq == 0, p_hi.astype(F32), 0.0)
                shift = jnp.where(rowq == 1, p_mid.astype(F32), shift)
                shift = jnp.where(rowq == 2, p_lo.astype(F32), shift)
                shift = jnp.where(rowq == 3, 1.0, shift)
                at = pl.multiple_of(base + half + 48, 16)
                qa_ref[pl.ds(at, HD), cols] = shift.astype(BF16)

        return carry

    lax.fori_loop(0, H, prep, 0)

    def first_stage(p, j):
        side, t, slot = j // NQ, j % NQ, j % 2
        h = 2 * p + side
        lanes = pl.ds(pl.multiple_of(p * 128, 128), 128)
        rhs = qa_ref[pl.ds(pl.multiple_of(h * 128, 128), 128), t * QB : (t + 1) * QB]
        s = mm(ka_ref[:, lanes], rhs)
        e_ref[slot] = jnp.exp2(s).astype(BF16)

    def second_stage(p, j):
        side, t, slot = j // NQ, j % NQ, j % 2
        h = 2 * p + side
        cols = slice(t * QB, (t + 1) * QB)
        lanes = pl.ds(pl.multiple_of(p * 128, 128), 128)
        hrows = pl.ds(pl.multiple_of(h * HD, HD), HD)
        krows = pl.ds(pl.multiple_of(C + h * HD, HD), HD)
        vrows = pl.ds(pl.multiple_of(2 * C + h * HD, HD), HD)
        o_un = mm(vt_ref[pl.ds(pl.multiple_of(h * 32, 32), 32), :], e_ref[slot])
        l_inv = 1.0 / o_un[HD : HD + 1, :]
        o = o_un[:HD, :] * l_inv
        live = (iota((HD, QB), 1) + t * QB) < n_live
        attT_ref[hrows, cols] = jnp.where(live, o, 0.0).astype(BF16)
        do = doT_ref[hrows, cols].astype(F32)
        dl = do * l_inv
        d_hi = dl.astype(BF16)
        d_lo = (dl - d_hi.astype(F32)).astype(BF16)
        cross = -jnp.sum(dl * o, axis=0, keepdims=True)
        c_hi, c_mid, c_lo = split3(cross)
        row = iota((32, QB), 0)
        tail = jnp.where(row == 0, c_hi.astype(F32), 0.0)
        tail = jnp.where(row == 1, c_mid.astype(F32), tail)
        tail = jnp.where(row == 2, c_lo.astype(F32), tail)
        both = jnp.concatenate([d_hi, d_lo], axis=0)
        zeros = jnp.zeros((64, QB), BF16)
        parts = [both, tail.astype(BF16)]
        parts = parts + [zeros] if side == 0 else [zeros] + parts
        dp = mm(va_ref[:, lanes], jnp.concatenate(parts, axis=0))
        ds_ref[...] = (e_ref[slot].astype(F32) * dp).astype(BF16)
        dv = mm_nt(both, e_ref[slot])
        dv = dv[:HD] + dv[HD:]
        dq = mm(pT_ref[krows, :], ds_ref[...])
        gpT_ref[hrows, cols] = (dq * SCALE).astype(BF16)
        dk = mm_nt(pT_ref[hrows, cols], ds_ref[...])
        if t == 0:
            dk_ref[...] = dk
            dv_ref[...] = dv
        elif t < NQ - 1:
            dk_ref[...] += dk
            dv_ref[...] += dv
        else:
            gpT_ref[krows, :] = ((dk_ref[...] + dk) * SCALE).astype(BF16)
            gpT_ref[vrows, :] = (dv_ref[...] + dv).astype(BF16)

    first_stage(0, 0)

    def pair(p, carry):
        for j in range(2 * NQ):
            if j < 2 * NQ - 1:
                first_stage(p, j + 1)
            else:
                first_stage(jnp.minimum(p + 1, H // 2 - 1), 0)
            second_stage(p, j)
        return carry

    lax.fori_loop(0, H // 2, pair, 0)

    grad_ref[: 3 * C, :] = mm(gpT_ref[...], hid_ref[...]) * POINT_SCALE
    grad_ref[3 * C :, :] = mm(attT_ref[...], og_ref[...]) * POINT_SCALE
    for half in range(2):
        part = grad_ref[:, half * 128 : (half + 1) * 128].reshape(128, 8, 128)
        send_ref[:, half * 8 : (half + 1) * 8, :] = part.astype(BF16)

    gain_sum = jnp.zeros((1, C), F32)
    for t in range(4):
        rows = pl.ds(t * QB, QB)
        att = jnp.transpose(attT_ref[:, rows])
        bo = gath_ref[rows, :].astype(F32) + mm(att, wproj_ref[...])
        bo_ref[rows, :] = bo.astype(BF16).astype(F32)
        gp = jnp.transpose(gpT_ref[:, rows])
        gh = mm_nt(gp, wqkv_ref[...])
        normed = normed_ref[rows, :]
        gain_sum = gain_sum + jnp.sum(gh * normed, axis=0, keepdims=True)
        g = gh * gain
        mean_g = jnp.mean(g, axis=1, keepdims=True)
        mean_c = jnp.mean(g * normed, axis=1, keepdims=True)
        dx = og_ref[rows, :].astype(F32) + inv_ref[rows, :] * (g - mean_g - normed * mean_c)
        dx_ref[rows, :] = dx.astype(BF16)
    gain_sum = gain_sum * POINT_SCALE
    gsum_ref[0] = gain_sum[:, :128]
    gsum_ref[1] = gain_sum[:, 128:]
    for t in range(4):
        spot = iota((QB, N), 0) + t * QB
        onehot = jnp.where(spot == serial_row, 1.0, 0.0).astype(BF16)
        gfeats_ref[pl.ds(t * QB, QB), :] = mm(onehot, dx_ref[...]).astype(BF16)

    ids = jnp.transpose(jnp.broadcast_to(cluster_ref[...].astype(F32), (128, N)))
    row = iota((N, 128), 0)
    down_ok, up_ok = [], []
    for step in (1, 2, 4):
        down_ok.append((pltpu.roll(ids, step, 0) == ids) & (row >= step))
        up_ok.append((pltpu.roll(ids, N - step, 0) == ids) & (row < N - step))
    for half in range(2):
        cols = slice(half * 128, (half + 1) * 128)
        m = bo_ref[:, cols]
        for i, step in enumerate((1, 2, 4)):
            m = jnp.maximum(m, jnp.where(down_ok[i], pltpu.roll(m, step, 0), -jnp.inf))
        for i, step in enumerate((1, 2, 4)):
            m = jnp.maximum(m, jnp.where(up_ok[i], pltpu.roll(m, N - step, 0), -jnp.inf))
        pooled_ref[:, cols] = m.astype(BF16)
        edge_ref[0, :, cols] = m[:8]
        edge_ref[1, :, cols] = m[N - 8 :]


def local_part(raw, serial, counts, gain, w_qkv, w_proj, out_grad, cluster):
    shapes = (
        jax.ShapeDtypeStruct((N, C), BF16),
        jax.ShapeDtypeStruct((N, C), BF16),
        jax.ShapeDtypeStruct((128, 16, 128), BF16),
        jax.ShapeDtypeStruct((2, 1, 128), F32),
        jax.ShapeDtypeStruct((2, 8, C), F32),
    )
    vm = pl.BlockSpec(memory_space=VMEM)
    sm = pl.BlockSpec(memory_space=pltpu.SMEM)
    return pl.pallas_call(
        local_kernel,
        out_shape=shapes,
        in_specs=[vm, vm, sm, vm, vm, vm, vm, vm],
        out_specs=[vm] * 5,
        scratch_shapes=[
            VMEM((N, C), BF16),
            VMEM((N, C), BF16),
            VMEM((N, C), F32),
            VMEM((N, 1), F32),
            VMEM((3 * C, N), BF16),
            VMEM((C, N), BF16),
            VMEM((N, 4 * C), BF16),
            VMEM((N, 4 * C), BF16),
            VMEM((H * 128, N), BF16),
            VMEM((H * 32, N), BF16),
            VMEM((2, N, QB), BF16),
            VMEM((N, QB), BF16),
            VMEM((C, N), BF16),
            VMEM((3 * C, N), BF16),
            VMEM((HD, N), F32),
            VMEM((HD, N), F32),
            VMEM((N, C), F32),
            VMEM((N, C), BF16),
            VMEM((N, C), F32),
        ],
        compiler_params=pltpu.CompilerParams(vmem_limit_bytes=56 * 1024 * 1024),
        name="local_part",
    )(raw, serial, counts, gain, w_qkv, w_proj, out_grad, cluster)


def comm_kernel(
    send_ref,
    gsum_ref,
    edge_ref,
    pooled_in_ref,
    cluster_ref,
    joined_ref,
    pooled_ref,
    gqkv_ref,
    gproj_ref,
    ggain_ref,
    pair_buf,
    pair_gain,
    edge_buf,
    chip_buf,
    chip_gain,
    rs_buf,
    gain_buf,
    ag_buf,
    out_buf,
    gain_out,
    grad_buf,
    sems,
):
    y = lax.axis_index("order_0")
    x = lax.axis_index("order_1")
    core = lax.axis_index("order_2")
    z = lax.axis_index("help")
    chip = (y * 4 + x) * 4 + z
    shard = ((y * 4 + x) * 2 + core) * 4 + z

    def of_shard(s):
        return (s // 32, (s // 8) % 4, (s // 4) % 2, s % 4)

    def of_chip(r):
        return ((y + r // 16) % 4, (x + (r // 4) % 4) % 4, core, (z + r % 4) % 4)

    partner = (y, x, 1 - core, z)
    following = of_shard((shard + 1) % 128)
    previous = of_shard((shard + 127) % 128)

    barrier = pltpu.get_barrier_semaphore()

    def greet(r, carry):
        pl.semaphore_signal(barrier, inc=1, device_id=of_chip(r), device_id_type=MESH)
        return carry

    lax.fori_loop(1, 64, greet, 0)
    for other in (partner, following, previous):
        pl.semaphore_signal(barrier, inc=1, device_id=other, device_id_type=MESH)
    pl.semaphore_wait(barrier, 66)

    def remote(src, dst, i, device):
        return pltpu.make_async_remote_copy(
            src_ref=src,
            dst_ref=dst,
            send_sem=sems.at[2 * i],
            recv_sem=sems.at[2 * i + 1],
            device_id=device,
            device_id_type=MESH,
        )

    far = 64 * (1 - core)
    pair_copy = remote(send_ref.at[pl.ds(far, 64)], pair_buf, 0, partner)
    pair_copy.start()
    pair_gain_copy = remote(gsum_ref.at[1 - core], pair_gain, 1, partner)
    pair_gain_copy.start()
    ahead = remote(edge_ref.at[1], edge_buf.at[0], 2, following)
    ahead.start()
    back = remote(edge_ref.at[0], edge_buf.at[1], 3, previous)
    back.start()

    pair_copy.wait()
    mine = send_ref[pl.ds(64 * core, 64)].astype(F32) + pair_buf[...].astype(F32)
    chip_buf[...] = mine.astype(BF16)
    pair_gain_copy.wait()
    chip_gain[...] = gsum_ref[core] + pair_gain[...]

    def scatter(r, carry):
        to = of_chip(r)
        other = (to[0] * 4 + to[1]) * 4 + to[3]
        remote(chip_buf.at[other], rs_buf.at[chip], 4, to).start()
        remote(chip_gain, gain_buf.at[chip], 5, to).start()
        return carry

    lax.fori_loop(1, 64, scatter, 0)
    rs_buf[pl.ds(chip, 1)] = chip_buf[pl.ds(chip, 1)]
    gain_buf[pl.ds(chip, 1)] = chip_gain[...][None]

    ahead.wait()
    back.wait()
    ids = jnp.transpose(jnp.broadcast_to(cluster_ref[...].astype(F32), (128, N)))
    first = ids[:8]
    last = ids[N - 8 :]
    pooled_ref[...] = pooled_in_ref[...]
    row = iota((8, 128), 0)
    linked = (joined_ref[...] > 0) & (shard > 0)
    head_ok = (first == first[:1]) & linked
    next_joined = edge_buf[1, 8:9, :128] > 0.0
    tail_ok = (last == last[7:8]) & next_joined & (shard < 127)
    for half in range(2):
        cols = slice(half * 128, (half + 1) * 128)
        from_prev = edge_buf[0, 7:8, cols]
        from_next = edge_buf[1, 0:1, cols]
        top = edge_ref[0, 0:8, cols]
        top = jnp.where(head_ok, jnp.maximum(top, from_prev), top)
        low = edge_ref[1, 0:8, cols]
        low = jnp.where(tail_ok, jnp.maximum(low, from_next), low)
        pooled_ref[0:16, cols] = jnp.concatenate(
            [top, pooled_in_ref[8:16, cols].astype(F32)], axis=0
        ).astype(BF16)
        pooled_ref[N - 16 : N, cols] = jnp.concatenate(
            [pooled_in_ref[N - 16 : N - 8, cols].astype(F32), low], axis=0
        ).astype(BF16)

    everything = pl.ds(0, 63)
    for i, (src, dst) in ((4, (ag_buf, rs_buf)), (5, (gain_out, gain_buf))):
        whole = remote(dst.at[everything], dst.at[everything], i, partner)
        whole.wait_recv()
        whole.wait_send()
    total = jnp.sum(rs_buf[...].astype(F32), axis=0)
    ag_buf[pl.ds(chip, 1)] = total.astype(BF16)[None]

    def gather(r, carry):
        remote(ag_buf.at[chip], ag_buf.at[chip], 6, of_chip(r)).start()
        return carry

    lax.fori_loop(1, 64, gather, 0)
    gain_out[pl.ds(core, 1)] = jnp.sum(gain_buf[...], axis=0)[None]
    last_gain = remote(gain_out.at[core], gain_out.at[core], 7, partner)
    last_gain.start()
    whole = remote(ag_buf.at[everything], ag_buf.at[everything], 6, partner)
    whole.wait_recv()
    whole.wait_send()
    last_copy = remote(ag_buf, out_buf.at[core], 8, partner)
    last_copy.start()
    out_buf[pl.ds(core, 1)] = ag_buf[...][None]
    last_gain.wait()
    ggain_ref[:, :128] = gain_out[0]
    ggain_ref[:, 128:] = gain_out[1]
    last_copy.wait()
    for c in range(2):
        for half in range(2):
            part = out_buf[c, :, half * 8 : (half + 1) * 8, :].astype(F32).reshape(512, 128)
            grad_buf[c * 512 : (c + 1) * 512, half * 128 : (half + 1) * 128] = part
    gqkv_ref[...] = jnp.transpose(grad_buf[: 3 * C, :])
    gproj_ref[...] = grad_buf[3 * C :, :]


def comm_part(send, gsum, edge, pooled, cluster, joined):
    shapes = (
        jax.ShapeDtypeStruct((N, C), BF16),
        jax.ShapeDtypeStruct((C, 3 * C), F32),
        jax.ShapeDtypeStruct((C, C), F32),
        jax.ShapeDtypeStruct((1, C), F32),
    )
    vm = pl.BlockSpec(memory_space=VMEM)
    return pl.pallas_call(
        comm_kernel,
        out_shape=shapes,
        in_specs=[vm] * 6,
        out_specs=[vm] * 4,
        scratch_shapes=[
            VMEM((64, 16, 128), BF16),
            VMEM((1, 128), F32),
            VMEM((2, 16, C), F32),
            VMEM((64, 16, 128), BF16),
            VMEM((1, 128), F32),
            VMEM((64, 16, 128), BF16),
            VMEM((64, 1, 128), F32),
            VMEM((64, 16, 128), BF16),
            VMEM((2, 64, 16, 128), BF16),
            VMEM((2, 1, 128), F32),
            VMEM((N, C), F32),
            pltpu.SemaphoreType.DMA((18,)),
        ],
        compiler_params=pltpu.CompilerParams(
            collective_id=0, has_side_effects=True, vmem_limit_bytes=32 * 1024 * 1024
        ),
        name="comm_part",
    )(send, gsum, edge, pooled, cluster, joined)


def body(raw_feats, serial, counts, norm_gain, w_qkv, w_proj, out_grad, cluster, joined):
    pooled, grad_feats, send, gsum, edge = local_part(
        raw_feats[0], serial, counts, norm_gain[None], w_qkv, w_proj, out_grad[0], cluster
    )
    flag = jnp.broadcast_to(joined[:, None], (8, C)).astype(F32)
    edge = jnp.concatenate([edge, jnp.broadcast_to(flag, (2, 8, C))], axis=1)
    flags = jnp.broadcast_to(joined[:, None], (1, 128))
    pooled, grad_qkv, grad_proj, grad_gain = comm_part(send, gsum, edge, pooled, cluster, flags)
    return (pooled[None], grad_feats[None], grad_qkv, grad_proj, grad_gain[0])


def solution(mesh):
    torus = Mesh(
        mesh.devices.reshape(4, 4, 2, mesh.shape["help"]), ("order_0", "order_1", "order_2", "help")
    )
    placed = (
        P(ORDER_HELP, None, None),
        P(ORDER_HELP, None),
        P(ORDER_HELP, None),
        P(),
        P(),
        P(),
        P(ORDER_HELP, None, None),
        P(ORDER_HELP, None),
        P(ORDER_HELP),
    )
    return jax.shard_map(
        body,
        mesh=torus,
        in_specs=placed,
        out_specs=(P(ORDER_HELP, None, None), P(ORDER_HELP, None, None), P(), P(), P()),
        check_vma=False,
    )
```

time: 458 us -> 122 us (0.27)
  starting transfers between devices: 263 us -> 0 us
  Pallas kernels: 0 us -> 113 us
  matrix products: 79.2 us -> 0 us
  local copies, waits for them, and re-layouts: 51.2 us -> 5.77 us
  other arithmetic: 33.1 us -> 0 us
  waiting for transfers between devices: 19.2 us -> 0 us
  loops' own time: 9.04 us -> 0 us
    all_to_all x4 -> x0, starting transfers between devices: 256 us -> none  [the longest x1 239 us: sent_and_summed(): lax.all_to_all(split_up(array, dim, devices), axis, 0, 0, tiled=True)]
    pallas_call x0 -> x2, Pallas kernels: none -> 113 us  [the longest x1 80 us: local_part(): pl.pallas_call(local_kernel, out_shape=shapes, in_specs=[vm, vm, sm, vm,...]
    dot_general x30 -> x0, matrix products: 62.5 us -> none  [the longest x12 31.8 us: head_block(): jnp.einsum('hqk,khd->qhd', weights, value_rows, preferred_element_type=jn...]
    all_to_all x4 -> x0, waiting for transfers between devices: 19.2 us -> none  [the longest x2 16.2 us: sent_to_all(): return lax.all_to_all(copies, axis, split_axis=0, concat_axis=0, tiled=True)]
    sub x4 -> x0, matrix products: 16.8 us -> none  [head_block(): exp_terms = jnp.exp(scores - row_peak)]
    reduce_sum x12 -> x0, other arithmetic: 16.6 us -> none  [the longest x4 9.27 us: head_block(): exp_terms = jnp.exp(scores - row_peak)]
    another operation x8 -> x0, local copies, waits for them, and re-layouts: 12.1 us -> none
    squeeze x12 -> x0, local copies, waits for them, and re-layouts: 10.7 us -> none  [attend_patch(): mixed_out = lax.map(one_block, blocks)]
  transfers between devices with their start and end apart: 6 -> 0, of which waited for: 3 -> 0; matrix products, arithmetic and copies ran while one was open for 5% -> 0% of each run, Pallas kernels for 0% -> 0%
where the time goes in v1:
time: 122 us; the launch traced here: 121 us
  Pallas kernels  113 us (93%)
  local copies, waits for them, and re-layouts  5.77 us (5%)
  between operations  1.95 us (2%)
    pallas_call x1, Pallas kernels, local_part(): pl.pallas_call(local_kernel, out_shape=shapes, in_specs=[vm, vm, sm, vm,...  80 us
    pallas_call x1, Pallas kernels, comm_part(): pl.pallas_call(comm_kernel, out_shape=shapes, in_specs=[vm] * 6, out_spec...  33 us
    unnamed x12, local copies, waits for them, and re-layouts  5.02 us

profile of v1, /device:TPU:1, one launch (start us, length us, event | category | flops | bytes accessed | tf_op | source)
XLA Modules:
  0.0 120.7 jit_solution(9596294612357358095)
XLA Ops:
  1.9 80.0 %local_part.1 = (bf16[1024,256]{1,0:T(8,128)(2,1)}, bf16[1024,256]{1,0:T(8,128)(2,1)}, bf16[128,16,128]{2,1,0:T(8,128)(2,1)}, f32[2,1,128]{2,1,0:T(1,128)}, f32[2,8,256]{2,1,0:T(8,128)}) custom-call(bf16[1024,256]{1,0:T(8,128)(2,1)} %bitcast.11, s32[1,1024]{1,0:T(1,128)} %serial_ref.1, s32[1,1]{1,0:T(1,128)S(6)} %copy.18.counts_ref, f32[1,256]{1,0:T(1,128)} %bitcast.13, ...), custom_call_target="tpu_custom_call" | custom-call | tf_op jit(solution)/shard_map/local_part/pallas_call | solution.py:300
  81.9 0.0 copy-start.2
  81.9 0.0 copy-start.3
  81.9 0.7 concatenate.3.edge_ref
  82.7 0.0 copy-done.2
  82.7 0.0 copy-done.3
  82.7 0.0 copy-start
  82.7 1.0 copy-done
  83.7 0.0 copy-start.1
  83.7 1.0 copy-done.1
  84.8 33.0 %comm_part.1 = (bf16[1024,256]{1,0:T(8,128)(2,1)S(1)}, f32[256,768]{1,0:T(8,128)S(1)}, f32[256,256]{1,0:T(8,128)S(1)}, f32[1,256]{1,0:T(1,128)S(1)}) custom-call(bf16[128,16,128]{2,1,0:T(8,128)(2,1)S(1)} %copy-done.1, f32[2,1,128]{2,1,0:T(1,128)S(1)} %copy-done.3, f32[2,16,256]{2,1,0:T(8,128)S(1)} %concatenate.3.edge_ref, bf16[1024,256]{1,0:T(8,128)(2,1)S(1)} %copy-done, ...), custom_call_target="tpu_custom_call" | custom-call | tf_op jit(solution)/shard_map/comm_part/pallas_call | solution.py:488
  117.7 0.8 copy.20
  118.5 0.9 copy.21
  119.4 0.7 copy.22
  120.1 0.6 copy.23
  (1 shorter events, 0.0 us)
Async XLA Ops:
  81.9 0.8 copy-start.2
  81.9 0.8 copy-start.3
  82.7 1.0 copy-start
  83.7 1.0 copy-start.1

commit v2 on v1

--- a/solution.py
+++ b/solution.py
@@ -14,6 +14,9 @@
 HD = 16
 QB = 256
 NQ = N // QB
+AQ = 512
+NA = N // AQ
+LAG = True
 GROUP = 8
 ORDER_HELP = ("order_0", "order_1", "order_2", "help")
 EPS = 1e-05
@@ -56,6 +59,7 @@
     wproj_ref,
     og_ref,
     cluster_ref,
+    joined_ref,
     pooled_ref,
     gfeats_ref,
     send_ref,
@@ -80,16 +84,20 @@
     grad_ref,
     dx_ref,
     bo_ref,
+    bo2_ref,
+    ids_ref,
+    cols_ref,
+    kv_ref,
 ):
     n_live = counts_ref[0, 0]
     gain = gain_ref[...]
     serial_row = serial_ref[...]
-    serial_cols = jnp.transpose(jnp.broadcast_to(serial_row.astype(F32), (128, N)))
+    cols_ref[...] = jnp.transpose(jnp.broadcast_to(serial_row.astype(F32), (128, N)))
     lane128 = iota((QB, 128), 1).astype(F32)
 
     for t in range(4):
         rows = pl.ds(t * QB, QB)
-        sc = serial_cols[t * QB : (t + 1) * QB]
+        sc = cols_ref[rows, :]
         onehot = jnp.concatenate(
             [jnp.where(sc == lane128 + float(128 * b), 1.0, 0.0).astype(BF16) for b in range(8)],
             axis=1,
@@ -109,24 +117,26 @@
         bpT = jnp.transpose(bp)
         lane = iota((C, QB), 1) + t * QB
         doT_ref[:, rows] = jnp.where(lane < n_live, bpT.astype(F32), 0.0).astype(BF16)
-        key_live = (iota((QB, C), 0) + t * QB) < n_live
-        kcols = packed[:, C : 2 * C]
-        vcols = packed[:, 2 * C :]
-        for b in range(4):
-            cols = pl.ds(b * C, C)
-            chan = iota((C, C), 0)
-            place = iota((C, C), 1)
-            spot = place % 64
-            same = ((place // 64 + 4 * b) == chan // HD) & (spot % HD == chan % HD)
-            rep_k = jnp.where(same & (spot < 3 * HD), 1.0, 0.0).astype(BF16)
-            rep_v = jnp.where(same & (spot < 2 * HD), 1.0, 0.0).astype(BF16)
-            spot_r = iota((QB, C), 1) % 64
-            ka = mm(kcols, rep_k)
-            ka = jnp.where((spot_r >= 48) & (spot_r < 51), 1.0, ka)
-            ka = jnp.where((spot_r == 51) & jnp.logical_not(key_live), NEG, ka)
+        kv_ref[rows, :] = packed[:, C:]
+
+    chan = iota((C, C), 0)
+    place = iota((C, C), 1)
+    spot = place % 64
+    for b in range(4):
+        cols = pl.ds(b * C, C)
+        same = ((place // 64 + 4 * b) == chan // HD) & (spot % HD == chan % HD)
+        rep_k = jnp.where(same & (spot < 3 * HD), 1.0, 0.0).astype(BF16)
+        rep_v = jnp.where(same & (spot < 2 * HD), 1.0, 0.0).astype(BF16)
+        spot_r = iota((1, C), 1) % 64
+        ones_k = jnp.where((spot_r >= 48) & (spot_r < 51), 1.0, 0.0)
+        ones_v = jnp.where((spot_r >= 32) & (spot_r < 35), 1.0, 0.0)
+        dead_k = jnp.where(spot_r == 51, NEG, 0.0)
+        for t in range(4):
+            rows = pl.ds(t * QB, QB)
+            dead = jnp.where((iota((QB, 1), 0) + t * QB) < n_live, 0.0, 1.0)
+            ka = mm(kv_ref[rows, :C], rep_k) + ones_k + dead * dead_k
             ka_ref[rows, cols] = ka.astype(BF16)
-            va = mm(vcols, rep_v)
-            va = jnp.where((spot_r >= 32) & (spot_r < 35), 1.0, va)
+            va = mm(kv_ref[rows, C:], rep_v) + ones_v
             va_ref[rows, cols] = va.astype(BF16)
 
     def prep(h, carry):
@@ -175,26 +185,30 @@
 
     lax.fori_loop(0, H, prep, 0)
 
-    def first_stage(p, j):
-        side, t, slot = j // NQ, j % NQ, j % 2
+    def names(p, j):
+        side, t, slot = j // NA, j % NA, j % 2
         h = 2 * p + side
-        lanes = pl.ds(pl.multiple_of(p * 128, 128), 128)
-        rhs = qa_ref[pl.ds(pl.multiple_of(h * 128, 128), 128), t * QB : (t + 1) * QB]
-        s = mm(ka_ref[:, lanes], rhs)
-        e_ref[slot] = jnp.exp2(s).astype(BF16)
-
-    def second_stage(p, j):
-        side, t, slot = j // NQ, j % NQ, j % 2
-        h = 2 * p + side
-        cols = slice(t * QB, (t + 1) * QB)
-        lanes = pl.ds(pl.multiple_of(p * 128, 128), 128)
         hrows = pl.ds(pl.multiple_of(h * HD, HD), HD)
         krows = pl.ds(pl.multiple_of(C + h * HD, HD), HD)
         vrows = pl.ds(pl.multiple_of(2 * C + h * HD, HD), HD)
-        o_un = mm(vt_ref[pl.ds(pl.multiple_of(h * 32, 32), 32), :], e_ref[slot])
+        lanes = pl.ds(pl.multiple_of(p * 128, 128), 128)
+        return side, t, slot, h, slice(t * AQ, (t + 1) * AQ), lanes, hrows, krows, vrows
+
+    def first_stage(p, j):
+        side, t, slot, h, cols, lanes, hrows, krows, vrows = names(p, j)
+        rhs = qa_ref[pl.ds(pl.multiple_of(h * 128, 128), 128), cols]
+        s = mm(ka_ref[:, lanes], rhs)
+        e_ref[slot] = jnp.exp2(s).astype(BF16)
+
+    def outputs(p, j):
+        side, t, slot, h, cols, lanes, hrows, krows, vrows = names(p, j)
+        return mm(vt_ref[pl.ds(pl.multiple_of(h * 32, 32), 32), :], e_ref[slot])
+
+    def cotangents(p, j, o_un):
+        side, t, slot, h, cols, lanes, hrows, krows, vrows = names(p, j)
         l_inv = 1.0 / o_un[HD : HD + 1, :]
         o = o_un[:HD, :] * l_inv
-        live = (iota((HD, QB), 1) + t * QB) < n_live
+        live = (iota((HD, AQ), 1) + t * AQ) < n_live
         attT_ref[hrows, cols] = jnp.where(live, o, 0.0).astype(BF16)
         do = doT_ref[hrows, cols].astype(F32)
         dl = do * l_inv
@@ -202,43 +216,68 @@
         d_lo = (dl - d_hi.astype(F32)).astype(BF16)
         cross = -jnp.sum(dl * o, axis=0, keepdims=True)
         c_hi, c_mid, c_lo = split3(cross)
-        row = iota((32, QB), 0)
+        row = iota((32, AQ), 0)
         tail = jnp.where(row == 0, c_hi.astype(F32), 0.0)
         tail = jnp.where(row == 1, c_mid.astype(F32), tail)
         tail = jnp.where(row == 2, c_lo.astype(F32), tail)
         both = jnp.concatenate([d_hi, d_lo], axis=0)
-        zeros = jnp.zeros((64, QB), BF16)
+        zeros = jnp.zeros((64, AQ), BF16)
         parts = [both, tail.astype(BF16)]
         parts = parts + [zeros] if side == 0 else [zeros] + parts
         dp = mm(va_ref[:, lanes], jnp.concatenate(parts, axis=0))
-        ds_ref[...] = (e_ref[slot].astype(F32) * dp).astype(BF16)
+        ds_ref[slot] = (e_ref[slot].astype(F32) * dp).astype(BF16)
+        return both
+
+    def value_grad(p, j, both):
+        side, t, slot, h, cols, lanes, hrows, krows, vrows = names(p, j)
         dv = mm_nt(both, e_ref[slot])
         dv = dv[:HD] + dv[HD:]
-        dq = mm(pT_ref[krows, :], ds_ref[...])
+        if t > 0:
+            dv = dv_ref[...] + dv
+        if t < NA - 1:
+            dv_ref[...] = dv
+        else:
+            gpT_ref[vrows, :] = dv.astype(BF16)
+
+    def score_grads(p, j):
+        side, t, slot, h, cols, lanes, hrows, krows, vrows = names(p, j)
+        dq = mm(pT_ref[krows, :], ds_ref[slot])
         gpT_ref[hrows, cols] = (dq * SCALE).astype(BF16)
-        dk = mm_nt(pT_ref[hrows, cols], ds_ref[...])
-        if t == 0:
+        dk = mm_nt(pT_ref[hrows, cols], ds_ref[slot])
+        if t > 0:
+            dk = dk_ref[...] + dk
+        if t < NA - 1:
             dk_ref[...] = dk
-            dv_ref[...] = dv
-        elif t < NQ - 1:
-            dk_ref[...] += dk
-            dv_ref[...] += dv
         else:
-            gpT_ref[krows, :] = ((dk_ref[...] + dk) * SCALE).astype(BF16)
-            gpT_ref[vrows, :] = (dv_ref[...] + dv).astype(BF16)
+            gpT_ref[krows, :] = (dk * SCALE).astype(BF16)
 
     first_stage(0, 0)
+    if LAG:
+        ds_ref[1] = jnp.zeros((N, AQ), BF16)
+        dk_ref[...] = jnp.zeros((HD, N), F32)
 
     def pair(p, carry):
-        for j in range(2 * NQ):
-            if j < 2 * NQ - 1:
+        for j in range(2 * NA):
+            o_un = outputs(p, j)
+            if j < 2 * NA - 1:
                 first_stage(p, j + 1)
             else:
                 first_stage(jnp.minimum(p + 1, H // 2 - 1), 0)
-            second_stage(p, j)
+            both = cotangents(p, j, o_un)
+            if LAG:
+                if j > 0:
+                    score_grads(p, j - 1)
+                else:
+                    score_grads(jnp.maximum(p - 1, 0), 2 * NA - 1)
+                value_grad(p, j, both)
+            else:
+                value_grad(p, j, both)
+                score_grads(p, j)
         return carry
 
     lax.fori_loop(0, H // 2, pair, 0)
+    if LAG:
+        score_grads(H // 2 - 1, 2 * NA - 1)
 
     grad_ref[: 3 * C, :] = mm(gpT_ref[...], hid_ref[...]) * POINT_SCALE
     grad_ref[3 * C :, :] = mm(attT_ref[...], og_ref[...]) * POINT_SCALE
@@ -251,7 +290,7 @@
         rows = pl.ds(t * QB, QB)
         att = jnp.transpose(attT_ref[:, rows])
         bo = gath_ref[rows, :].astype(F32) + mm(att, wproj_ref[...])
-        bo_ref[rows, :] = bo.astype(BF16).astype(F32)
+        bo_ref[pl.ds(t * QB + 8, QB), :] = bo.astype(BF16).astype(F32)
         gp = jnp.transpose(gpT_ref[:, rows])
         gh = mm_nt(gp, wqkv_ref[...])
         normed = normed_ref[rows, :]
@@ -269,38 +308,54 @@
         onehot = jnp.where(spot == serial_row, 1.0, 0.0).astype(BF16)
         gfeats_ref[pl.ds(t * QB, QB), :] = mm(onehot, dx_ref[...]).astype(BF16)
 
-    ids = jnp.transpose(jnp.broadcast_to(cluster_ref[...].astype(F32), (128, N)))
-    row = iota((N, 128), 0)
-    down_ok, up_ok = [], []
-    for step in (1, 2, 4):
-        down_ok.append((pltpu.roll(ids, step, 0) == ids) & (row >= step))
-        up_ok.append((pltpu.roll(ids, N - step, 0) == ids) & (row < N - step))
-    for half in range(2):
-        cols = slice(half * 128, (half + 1) * 128)
-        m = bo_ref[:, cols]
-        for i, step in enumerate((1, 2, 4)):
-            m = jnp.maximum(m, jnp.where(down_ok[i], pltpu.roll(m, step, 0), -jnp.inf))
-        for i, step in enumerate((1, 2, 4)):
-            m = jnp.maximum(m, jnp.where(up_ok[i], pltpu.roll(m, N - step, 0), -jnp.inf))
-        pooled_ref[:, cols] = m.astype(BF16)
-        edge_ref[0, :, cols] = m[:8]
-        edge_ref[1, :, cols] = m[N - 8 :]
-
-
-def local_part(raw, serial, counts, gain, w_qkv, w_proj, out_grad, cluster):
+    ids_ref[8 : N + 8, :] = jnp.transpose(
+        jnp.broadcast_to(cluster_ref[...].astype(F32), (128, N))
+    )
+    ids_ref[:8, :] = jnp.full((8, 128), -1.0, F32)
+    ids_ref[N + 8 :, :] = jnp.full((8, 128), -2.0, F32)
+    bo_ref[:8, :] = jnp.full((8, C), -jnp.inf, F32)
+    bo_ref[N + 8 :, :] = jnp.full((8, C), -jnp.inf, F32)
+    span = 128
+    wide = span + 16
+
+    def pool(i, carry):
+        at = pl.multiple_of(i * span, span)
+        ids = ids_ref[pl.ds(at, wide), :]
+        for half in range(2):
+            cols = slice(half * 128, (half + 1) * 128)
+            m = bo_ref[pl.ds(at, wide), cols]
+            for step in (1, 2, 4):
+                ok = pltpu.roll(ids, step, 0) == ids
+                m = jnp.maximum(m, jnp.where(ok, pltpu.roll(m, step, 0), -jnp.inf))
+            for step in (1, 2, 4):
+                ok = pltpu.roll(ids, wide - step, 0) == ids
+                m = jnp.maximum(m, jnp.where(ok, pltpu.roll(m, wide - step, 0), -jnp.inf))
+            bo2_ref[pl.ds(at, span), cols] = m[8 : span + 8]
+        return carry
+
+    lax.fori_loop(0, N // span, pool, 0)
+    pooled_ref[...] = bo2_ref[...].astype(BF16)
+    edge_ref[0, :8, :] = bo2_ref[:8, :]
+    edge_ref[1, :8, :] = bo2_ref[N - 8 :, :]
+    flag = jnp.full((8, C), joined_ref[0], jnp.int32).astype(F32)
+    edge_ref[0, 8:, :] = flag
+    edge_ref[1, 8:, :] = flag
+
+
+def local_part(raw, serial, counts, gain, w_qkv, w_proj, out_grad, cluster, joined):
     shapes = (
         jax.ShapeDtypeStruct((N, C), BF16),
         jax.ShapeDtypeStruct((N, C), BF16),
         jax.ShapeDtypeStruct((128, 16, 128), BF16),
         jax.ShapeDtypeStruct((2, 1, 128), F32),
-        jax.ShapeDtypeStruct((2, 8, C), F32),
+        jax.ShapeDtypeStruct((2, 16, C), F32),
     )
     vm = pl.BlockSpec(memory_space=VMEM)
     sm = pl.BlockSpec(memory_space=pltpu.SMEM)
     return pl.pallas_call(
         local_kernel,
         out_shape=shapes,
-        in_specs=[vm, vm, sm, vm, vm, vm, vm, vm],
+        in_specs=[vm, vm, sm, vm, vm, vm, vm, vm, sm],
         out_specs=[vm] * 5,
         scratch_shapes=[
             VMEM((N, C), BF16),
@@ -313,29 +368,32 @@
             VMEM((N, 4 * C), BF16),
             VMEM((H * 128, N), BF16),
             VMEM((H * 32, N), BF16),
-            VMEM((2, N, QB), BF16),
-            VMEM((N, QB), BF16),
+            VMEM((2, N, AQ), BF16),
+            VMEM((2, N, AQ), BF16),
             VMEM((C, N), BF16),
             VMEM((3 * C, N), BF16),
             VMEM((HD, N), F32),
             VMEM((HD, N), F32),
             VMEM((N, C), F32),
             VMEM((N, C), BF16),
+            VMEM((N + 16, C), F32),
             VMEM((N, C), F32),
+            VMEM((N + 16, 128), F32),
+            VMEM((N, 128), F32),
+            VMEM((N, 2 * C), BF16),
         ],
         compiler_params=pltpu.CompilerParams(vmem_limit_bytes=56 * 1024 * 1024),
         name="local_part",
-    )(raw, serial, counts, gain, w_qkv, w_proj, out_grad, cluster)
+    )(raw, serial, counts, gain, w_qkv, w_proj, out_grad, cluster, joined)
 
 
 def comm_kernel(
     send_ref,
     gsum_ref,
     edge_ref,
-    pooled_in_ref,
+    ends_in_ref,
     cluster_ref,
-    joined_ref,
-    pooled_ref,
+    ends_ref,
     gqkv_ref,
     gproj_ref,
     ggain_ref,
@@ -422,9 +480,7 @@
     ids = jnp.transpose(jnp.broadcast_to(cluster_ref[...].astype(F32), (128, N)))
     first = ids[:8]
     last = ids[N - 8 :]
-    pooled_ref[...] = pooled_in_ref[...]
-    row = iota((8, 128), 0)
-    linked = (joined_ref[...] > 0) & (shard > 0)
+    linked = (edge_ref[0, 8:9, :128] > 0.0) & (shard > 0)
     head_ok = (first == first[:1]) & linked
     next_joined = edge_buf[1, 8:9, :128] > 0.0
     tail_ok = (last == last[7:8]) & next_joined & (shard < 127)
@@ -436,12 +492,10 @@
         top = jnp.where(head_ok, jnp.maximum(top, from_prev), top)
         low = edge_ref[1, 0:8, cols]
         low = jnp.where(tail_ok, jnp.maximum(low, from_next), low)
-        pooled_ref[0:16, cols] = jnp.concatenate(
-            [top, pooled_in_ref[8:16, cols].astype(F32)], axis=0
-        ).astype(BF16)
-        pooled_ref[N - 16 : N, cols] = jnp.concatenate(
-            [pooled_in_ref[N - 16 : N - 8, cols].astype(F32), low], axis=0
-        ).astype(BF16)
+        above = ends_in_ref[8:16, cols].astype(F32)
+        below = ends_in_ref[16:24, cols].astype(F32)
+        ends_ref[:16, cols] = jnp.concatenate([top, above], axis=0).astype(BF16)
+        ends_ref[16:, cols] = jnp.concatenate([below, low], axis=0).astype(BF16)
 
     everything = pl.ds(0, 63)
     for i, (src, dst) in ((4, (ag_buf, rs_buf)), (5, (gain_out, gain_buf))):
@@ -477,9 +531,9 @@
     gproj_ref[...] = grad_buf[3 * C :, :]
 
 
-def comm_part(send, gsum, edge, pooled, cluster, joined):
+def comm_part(send, gsum, edge, ends, cluster):
     shapes = (
-        jax.ShapeDtypeStruct((N, C), BF16),
+        jax.ShapeDtypeStruct((32, C), BF16),
         jax.ShapeDtypeStruct((C, 3 * C), F32),
         jax.ShapeDtypeStruct((C, C), F32),
         jax.ShapeDtypeStruct((1, C), F32),
@@ -488,7 +542,7 @@
     return pl.pallas_call(
         comm_kernel,
         out_shape=shapes,
-        in_specs=[vm] * 6,
+        in_specs=[vm] * 5,
         out_specs=[vm] * 4,
         scratch_shapes=[
             VMEM((64, 16, 128), BF16),
@@ -508,17 +562,16 @@
             collective_id=0, has_side_effects=True, vmem_limit_bytes=32 * 1024 * 1024
         ),
         name="comm_part",
-    )(send, gsum, edge, pooled, cluster, joined)
+    )(send, gsum, edge, ends, cluster)
 
 
 def body(raw_feats, serial, counts, norm_gain, w_qkv, w_proj, out_grad, cluster, joined):
     pooled, grad_feats, send, gsum, edge = local_part(
-        raw_feats[0], serial, counts, norm_gain[None], w_qkv, w_proj, out_grad[0], cluster
-    )
-    flag = jnp.broadcast_to(joined[:, None], (8, C)).astype(F32)
-    edge = jnp.concatenate([edge, jnp.broadcast_to(flag, (2, 8, C))], axis=1)
-    flags = jnp.broadcast_to(joined[:, None], (1, 128))
-    pooled, grad_qkv, grad_proj, grad_gain = comm_part(send, gsum, edge, pooled, cluster, flags)
+        raw_feats[0], serial, counts, norm_gain[None], w_qkv, w_proj, out_grad[0], cluster, joined
+    )
+    ends = jnp.concatenate([pooled[:16], pooled[N - 16 :]], axis=0)
+    ends, grad_qkv, grad_proj, grad_gain = comm_part(send, gsum, edge, ends, cluster)
+    pooled = pooled.at[:16].set(ends[:16]).at[N - 16 :].set(ends[16:])
     return (pooled[None], grad_feats[None], grad_qkv, grad_proj, grad_gain[0])
 
 

time: 122 us -> 116 us (0.951); the launches traced: 121 us -> 117 us
  Pallas kernels: 113 us -> 109 us
    pallas_call x1, Pallas kernels: 80 us -> 77 us  [local_part(): pl.pallas_call(local_kernel, out_shape=shapes, in_specs=[vm, vm, sm, vm,...]
    unnamed x12 -> x11, local copies, waits for them, and re-layouts: 5.02 us -> 3.88 us
where the time goes in v2:
time: 116 us; the launch traced here: 117 us
  Pallas kernels  109 us (94%)
  local copies, waits for them, and re-layouts  5.8 us (5%)
  between operations  1.94 us (2%)
    pallas_call x1, Pallas kernels, local_part(): pl.pallas_call(local_kernel, out_shape=shapes, in_specs=[vm, vm, sm, vm,...  77 us
    pallas_call x1, Pallas kernels, comm_part(): pl.pallas_call(comm_kernel, out_shape=shapes, in_specs=[vm] * 5, out_spec...  31.8 us
    unnamed x11, local copies, waits for them, and re-layouts  3.88 us

profile of v2, /device:TPU:1, one launch (start us, length us, event | category | flops | bytes accessed | tf_op | source)
XLA Modules:
  0.0 116.6 jit_solution(15372886431266036154)
XLA Ops:
  1.9 77.0 %local_part.1 = (bf16[1024,256]{1,0:T(8,128)(2,1)}, bf16[1024,256]{1,0:T(8,128)(2,1)}, bf16[128,16,128]{2,1,0:T(8,128)(2,1)}, f32[2,1,128]{2,1,0:T(1,128)}, f32[2,16,256]{2,1,0:T(8,128)}) custom-call(bf16[1024,256]{1,0:T(8,128)(2,1)} %bitcast.11, s32[1,1024]{1,0:T(1,128)} %serial_ref.1, s32[1,1]{1,0:T(1,128)S(6)} %copy.19.counts_ref, f32[1,256]{1,0:T(1,128)} %bitcast.13, ...), custom_call_target="tpu_custom_call" | custom-call | tf_op jit(solution)/shard_map/local_part/pallas_call | solution.py:355
  79.0 0.0 copy-start.1
  79.0 0.7 fusion
  79.7 0.0 copy-start.2
  79.7 0.0 copy-start.3
  79.7 0.1 copy-done.1
  79.7 0.6 copy-done.2
  80.4 0.0 copy-done.3
  80.4 0.0 copy-start
  80.4 1.0 copy-done
  81.4 31.8 %comm_part.1 = (bf16[32,256]{1,0:T(8,128)(2,1)S(1)}, f32[256,768]{1,0:T(8,128)S(1)}, f32[256,256]{1,0:T(8,128)S(1)}, f32[1,256]{1,0:T(1,128)S(1)}) custom-call(bf16[128,16,128]{2,1,0:T(8,128)(2,1)S(1)} %copy-done, f32[2,1,128]{2,1,0:T(1,128)S(1)} %copy-done.3, f32[2,16,256]{2,1,0:T(8,128)S(1)} %copy-done.1, bf16[32,256]{1,0:T(8,128)(2,1)S(1)} %pad_maximum_fusion.ends_in_ref, ...), custom_call_target="tpu_custom_call" | custom-call | tf_op jit(solution)/shard_map/comm_part/pallas_call | solution.py:542
  113.2 0.6 bitcast_dynamic-update-slice_fusion.1
  113.8 0.6 bitcast_dynamic-update-slice_fusion
  114.4 0.9 copy.21
  115.3 0.7 copy.22
  116.0 0.6 copy.23
  (1 shorter events, 0.0 us)
Async XLA Ops:
  79.0 0.8 copy-start.1
  79.7 0.7 copy-start.2
  79.7 0.7 copy-start.3
  80.4 1.0 copy-start

commit v3 on v2

--- a/solution.py
+++ b/solution.py
@@ -16,7 +16,7 @@
 NQ = N // QB
 AQ = 512
 NA = N // AQ
-LAG = True
+LAG = False
 GROUP = 8
 ORDER_HELP = ("order_0", "order_1", "order_2", "help")
 EPS = 1e-05
@@ -88,6 +88,8 @@
     ids_ref,
     cols_ref,
     kv_ref,
+    et_ref,
+    dst_ref,
 ):
     n_live = counts_ref[0, 0]
     gain = gain_ref[...]
@@ -198,7 +200,9 @@
         side, t, slot, h, cols, lanes, hrows, krows, vrows = names(p, j)
         rhs = qa_ref[pl.ds(pl.multiple_of(h * 128, 128), 128), cols]
         s = mm(ka_ref[:, lanes], rhs)
-        e_ref[slot] = jnp.exp2(s).astype(BF16)
+        e = jnp.exp2(s).astype(BF16)
+        e_ref[slot] = e
+        et_ref[slot] = jnp.transpose(e)
 
     def outputs(p, j):
         side, t, slot, h, cols, lanes, hrows, krows, vrows = names(p, j)
@@ -225,12 +229,14 @@
         parts = [both, tail.astype(BF16)]
         parts = parts + [zeros] if side == 0 else [zeros] + parts
         dp = mm(va_ref[:, lanes], jnp.concatenate(parts, axis=0))
-        ds_ref[slot] = (e_ref[slot].astype(F32) * dp).astype(BF16)
+        ds = (e_ref[slot].astype(F32) * dp).astype(BF16)
+        ds_ref[slot] = ds
+        dst_ref[slot] = jnp.transpose(ds)
         return both
 
     def value_grad(p, j, both):
         side, t, slot, h, cols, lanes, hrows, krows, vrows = names(p, j)
-        dv = mm_nt(both, e_ref[slot])
+        dv = mm(both, et_ref[slot])
         dv = dv[:HD] + dv[HD:]
         if t > 0:
             dv = dv_ref[...] + dv
@@ -243,7 +249,7 @@
         side, t, slot, h, cols, lanes, hrows, krows, vrows = names(p, j)
         dq = mm(pT_ref[krows, :], ds_ref[slot])
         gpT_ref[hrows, cols] = (dq * SCALE).astype(BF16)
-        dk = mm_nt(pT_ref[hrows, cols], ds_ref[slot])
+        dk = mm(pT_ref[hrows, cols], dst_ref[slot])
         if t > 0:
             dk = dk_ref[...] + dk
         if t < NA - 1:
@@ -254,6 +260,7 @@
     first_stage(0, 0)
     if LAG:
         ds_ref[1] = jnp.zeros((N, AQ), BF16)
+        dst_ref[1] = jnp.zeros((AQ, N), BF16)
         dk_ref[...] = jnp.zeros((HD, N), F32)
 
     def pair(p, carry):
@@ -381,6 +388,8 @@
             VMEM((N + 16, 128), F32),
             VMEM((N, 128), F32),
             VMEM((N, 2 * C), BF16),
+            VMEM((2, AQ, N), BF16),
+            VMEM((2, AQ, N), BF16),
         ],
         compiler_params=pltpu.CompilerParams(vmem_limit_bytes=56 * 1024 * 1024),
         name="local_part",

time: 116 us -> 104 us (0.90); the launches traced: 117 us -> 102 us
  Pallas kernels: 109 us -> 94.2 us
    pallas_call x1, Pallas kernels: 77 us -> 65.1 us  [local_part(): pl.pallas_call(local_kernel, out_shape=shapes, in_specs=[vm, vm, sm, vm,...]
    pallas_call x1, Pallas kernels: 31.8 us -> 29.1 us  [comm_part(): pl.pallas_call(comm_kernel, out_shape=shapes, in_specs=[vm] * 5, out_spec...]
where the time goes in v3:
time: 104 us; the launch traced here: 102 us
  Pallas kernels  94.2 us (91%)
  local copies, waits for them, and re-layouts  5.8 us (6%)
  between operations  1.94 us (2%)
    pallas_call x1, Pallas kernels, local_part(): pl.pallas_call(local_kernel, out_shape=shapes, in_specs=[vm, vm, sm, vm,...  65.1 us
    pallas_call x1, Pallas kernels, comm_part(): pl.pallas_call(comm_kernel, out_shape=shapes, in_specs=[vm] * 5, out_spec...  29.1 us
    unnamed x11, local copies, waits for them, and re-layouts  3.88 us

profile of v3, /device:TPU:1, one launch (start us, length us, event | category | flops | bytes accessed | tf_op | source)
XLA Modules:
  0.0 102.0 jit_solution(15329108797401388720)
XLA Ops:
  1.9 65.1 %local_part.1 = (bf16[1024,256]{1,0:T(8,128)(2,1)}, bf16[1024,256]{1,0:T(8,128)(2,1)}, bf16[128,16,128]{2,1,0:T(8,128)(2,1)}, f32[2,1,128]{2,1,0:T(1,128)}, f32[2,16,256]{2,1,0:T(8,128)}) custom-call(bf16[1024,256]{1,0:T(8,128)(2,1)} %bitcast.11, s32[1,1024]{1,0:T(1,128)} %serial_ref.1, s32[1,1]{1,0:T(1,128)S(6)} %copy.19.counts_ref, f32[1,256]{1,0:T(1,128)} %bitcast.13, ...), custom_call_target="tpu_custom_call" | custom-call | tf_op jit(solution)/shard_map/local_part/pallas_call | solution.py:362
  67.1 0.0 copy-start.1
  67.1 0.7 fusion
  67.8 0.0 copy-start.2
  67.8 0.0 copy-start.3
  67.8 0.1 copy-done.1
  67.9 0.6 copy-done.2
  68.5 0.0 copy-done.3
  68.5 0.0 copy-start
  68.5 1.0 %copy-done = bf16[128,16,128]{2,1,0:T(8,128)(2,1)S(1)} copy-done((bf16[128,16,128]{2,1,0:T(8,128)(2,1)S(1)}, bf16[128,16,128]{2,1,0:T(8,128)(2,1)}, u32[]{:S(2)}) %copy-start) | copy-done | bytes 524312
  69.5 29.1 %comm_part.1 = (bf16[32,256]{1,0:T(8,128)(2,1)S(1)}, f32[256,768]{1,0:T(8,128)S(1)}, f32[256,256]{1,0:T(8,128)S(1)}, f32[1,256]{1,0:T(1,128)S(1)}) custom-call(bf16[128,16,128]{2,1,0:T(8,128)(2,1)S(1)} %copy-done, f32[2,1,128]{2,1,0:T(1,128)S(1)} %copy-done.3, f32[2,16,256]{2,1,0:T(8,128)S(1)} %copy-done.1, bf16[32,256]{1,0:T(8,128)(2,1)S(1)} %pad_maximum_fusion.ends_in_ref, ...), custom_call_target="tpu_custom_call" | custom-call | tf_op jit(solution)/shard_map/comm_part/pallas_call | solution.py:551
  98.6 0.6 bitcast_dynamic-update-slice_fusion.1
  99.2 0.6 bitcast_dynamic-update-slice_fusion
  99.8 0.9 copy.21
  100.7 0.7 copy.22
  101.4 0.6 copy.23
  (1 shorter events, 0.0 us)
Async XLA Ops:
  67.1 0.8 copy-start.1
  67.8 0.7 copy-start.2
  67.8 0.7 copy-start.3
  68.5 1.0 %copy-start = (bf16[128,16,128]{2,1,0:T(8,128)(2,1)S(1)}, bf16[128,16,128]{2,1,0:T(8,128)(2,1)}, u32[]{:S(2)}) copy-start(bf16[128,16,128]{2,1,0:T(8,128)(2,1)} %get-tuple-element.39.send_ref) | copy-start | bytes 1572868

commit v4 on v2

--- a/solution.py
+++ b/solution.py
@@ -16,7 +16,8 @@
 NQ = N // QB
 AQ = 512
 NA = N // AQ
-LAG = True
+KC = 512
+NK = N // KC
 GROUP = 8
 ORDER_HELP = ("order_0", "order_1", "order_2", "help")
 EPS = 1e-05
@@ -88,6 +89,8 @@
     ids_ref,
     cols_ref,
     kv_ref,
+    et_ref,
+    dst_ref,
 ):
     n_live = counts_ref[0, 0]
     gain = gain_ref[...]
@@ -194,18 +197,20 @@
         lanes = pl.ds(pl.multiple_of(p * 128, 128), 128)
         return side, t, slot, h, slice(t * AQ, (t + 1) * AQ), lanes, hrows, krows, vrows
 
-    def first_stage(p, j):
+    def keys(r):
+        return slice(r * KC, (r + 1) * KC)
+
+    def first_stage(p, j, r):
         side, t, slot, h, cols, lanes, hrows, krows, vrows = names(p, j)
         rhs = qa_ref[pl.ds(pl.multiple_of(h * 128, 128), 128), cols]
-        s = mm(ka_ref[:, lanes], rhs)
-        e_ref[slot] = jnp.exp2(s).astype(BF16)
-
-    def outputs(p, j):
+        e = jnp.exp2(mm(ka_ref[keys(r), lanes], rhs)).astype(BF16)
+        e_ref[slot, keys(r), :] = e
+        et_ref[slot, :, keys(r)] = jnp.transpose(e)
+
+    def block(p, j, following):
         side, t, slot, h, cols, lanes, hrows, krows, vrows = names(p, j)
-        return mm(vt_ref[pl.ds(pl.multiple_of(h * 32, 32), 32), :], e_ref[slot])
-
-    def cotangents(p, j, o_un):
-        side, t, slot, h, cols, lanes, hrows, krows, vrows = names(p, j)
+        o_un = mm(vt_ref[pl.ds(pl.multiple_of(h * 32, 32), 32), :], e_ref[slot])
+        first_stage(*following, 0)
         l_inv = 1.0 / o_un[HD : HD + 1, :]
         o = o_un[:HD, :] * l_inv
         live = (iota((HD, AQ), 1) + t * AQ) < n_live
@@ -224,60 +229,58 @@
         zeros = jnp.zeros((64, AQ), BF16)
         parts = [both, tail.astype(BF16)]
         parts = parts + [zeros] if side == 0 else [zeros] + parts
-        dp = mm(va_ref[:, lanes], jnp.concatenate(parts, axis=0))
-        ds_ref[slot] = (e_ref[slot].astype(F32) * dp).astype(BF16)
-        return both
-
-    def value_grad(p, j, both):
-        side, t, slot, h, cols, lanes, hrows, krows, vrows = names(p, j)
-        dv = mm_nt(both, e_ref[slot])
-        dv = dv[:HD] + dv[HD:]
-        if t > 0:
-            dv = dv_ref[...] + dv
-        if t < NA - 1:
-            dv_ref[...] = dv
-        else:
-            gpT_ref[vrows, :] = dv.astype(BF16)
-
-    def score_grads(p, j):
-        side, t, slot, h, cols, lanes, hrows, krows, vrows = names(p, j)
-        dq = mm(pT_ref[krows, :], ds_ref[slot])
+        rhs = jnp.concatenate(parts, axis=0)
+
+        def value_grad(r):
+            dv = mm(both, et_ref[slot, :, keys(r)])
+            dv = dv[:HD] + dv[HD:]
+            if t > 0:
+                dv = dv_ref[:, keys(r)] + dv
+            if t < NA - 1:
+                dv_ref[:, keys(r)] = dv
+            else:
+                gpT_ref[vrows, keys(r)] = dv.astype(BF16)
+
+        def cotangent(r):
+            dp = mm(va_ref[keys(r), lanes], rhs)
+            ds = (e_ref[slot, keys(r), :].astype(F32) * dp).astype(BF16)
+            ds_ref[slot, keys(r), :] = ds
+            dst_ref[slot, :, keys(r)] = jnp.transpose(ds)
+
+        def score_grads(r):
+            dk = mm(pT_ref[hrows, cols], dst_ref[slot, :, keys(r)])
+            if t > 0:
+                dk = dk_ref[:, keys(r)] + dk
+            if t < NA - 1:
+                dk_ref[:, keys(r)] = dk
+            else:
+                gpT_ref[krows, keys(r)] = (dk * SCALE).astype(BF16)
+            return mm(pT_ref[krows, keys(r)], ds_ref[slot, keys(r), :])
+
+        for r in range(1, NK):
+            first_stage(*following, r)
+            value_grad(r - 1)
+        cotangent(0)
+        value_grad(NK - 1)
+        dq = jnp.zeros((HD, AQ), F32)
+        for r in range(1, NK):
+            cotangent(r)
+            dq = dq + score_grads(r - 1)
+        dq = dq + score_grads(NK - 1)
         gpT_ref[hrows, cols] = (dq * SCALE).astype(BF16)
-        dk = mm_nt(pT_ref[hrows, cols], ds_ref[slot])
-        if t > 0:
-            dk = dk_ref[...] + dk
-        if t < NA - 1:
-            dk_ref[...] = dk
-        else:
-            gpT_ref[krows, :] = (dk * SCALE).astype(BF16)
-
-    first_stage(0, 0)
-    if LAG:
-        ds_ref[1] = jnp.zeros((N, AQ), BF16)
-        dk_ref[...] = jnp.zeros((HD, N), F32)
+
+    for r in range(NK):
+        first_stage(0, 0, r)
 
     def pair(p, carry):
         for j in range(2 * NA):
-            o_un = outputs(p, j)
             if j < 2 * NA - 1:
-                first_stage(p, j + 1)
+                block(p, j, (p, j + 1))
             else:
-                first_stage(jnp.minimum(p + 1, H // 2 - 1), 0)
-            both = cotangents(p, j, o_un)
-            if LAG:
-                if j > 0:
-                    score_grads(p, j - 1)
-                else:
-                    score_grads(jnp.maximum(p - 1, 0), 2 * NA - 1)
-                value_grad(p, j, both)
-            else:
-                value_grad(p, j, both)
-                score_grads(p, j)
+                block(p, j, (jnp.minimum(p + 1, H // 2 - 1), 0))
         return carry
 
     lax.fori_loop(0, H // 2, pair, 0)
-    if LAG:
-        score_grads(H // 2 - 1, 2 * NA - 1)
 
     grad_ref[: 3 * C, :] = mm(gpT_ref[...], hid_ref[...]) * POINT_SCALE
     grad_ref[3 * C :, :] = mm(attT_ref[...], og_ref[...]) * POINT_SCALE
@@ -321,15 +324,13 @@
     def pool(i, carry):
         at = pl.multiple_of(i * span, span)
         ids = ids_ref[pl.ds(at, wide), :]
+        shifts = (1, 2, 4, wide - 1, wide - 2, wide - 4)
+        same = [pltpu.roll(ids, step, 0) == ids for step in shifts]
         for half in range(2):
             cols = slice(half * 128, (half + 1) * 128)
             m = bo_ref[pl.ds(at, wide), cols]
-            for step in (1, 2, 4):
-                ok = pltpu.roll(ids, step, 0) == ids
+            for step, ok in zip(shifts, same):
                 m = jnp.maximum(m, jnp.where(ok, pltpu.roll(m, step, 0), -jnp.inf))
-            for step in (1, 2, 4):
-                ok = pltpu.roll(ids, wide - step, 0) == ids
-                m = jnp.maximum(m, jnp.where(ok, pltpu.roll(m, wide - step, 0), -jnp.inf))
             bo2_ref[pl.ds(at, span), cols] = m[8 : span + 8]
         return carry
 
@@ -381,8 +382,10 @@
             VMEM((N + 16, 128), F32),
             VMEM((N, 128), F32),
             VMEM((N, 2 * C), BF16),
+            VMEM((2, AQ, N), BF16),
+            VMEM((2, AQ, N), BF16),
         ],
-        compiler_params=pltpu.CompilerParams(vmem_limit_bytes=56 * 1024 * 1024),
+        compiler_params=pltpu.CompilerParams(vmem_limit_bytes=46 * 1024 * 1024),
         name="local_part",
     )(raw, serial, counts, gain, w_qkv, w_proj, out_grad, cluster, joined)
 
@@ -559,7 +562,7 @@
             pltpu.SemaphoreType.DMA((18,)),
         ],
         compiler_params=pltpu.CompilerParams(
-            collective_id=0, has_side_effects=True, vmem_limit_bytes=32 * 1024 * 1024
+            collective_id=0, has_side_effects=True, vmem_limit_bytes=16 * 1024 * 1024
         ),
         name="comm_part",
     )(send, gsum, edge, ends, cluster)

time: 116 us -> 110 us (0.948)
  Pallas kernels: 109 us -> 99.5 us
  local copies, waits for them, and re-layouts: 5.8 us -> 8.7 us
    pallas_call x1, Pallas kernels: 77 us -> 63 us  [local_part(): pl.pallas_call(local_kernel, out_shape=shapes, in_specs=[vm, vm, sm, vm,...]
    pallas_call x1, Pallas kernels: 31.8 us -> 36.6 us  [comm_part(): pl.pallas_call(comm_kernel, out_shape=shapes, in_specs=[vm] * 5, out_spec...]
    unnamed x11 -> x17, local copies, waits for them, and re-layouts: 3.88 us -> 6.79 us
where the time goes in v4:
time: 110 us
  Pallas kernels  99.5 us (90%)
  local copies, waits for them, and re-layouts  8.7 us (8%)
  between operations  2.01 us (2%)
    pallas_call x1, Pallas kernels, local_part(): pl.pallas_call(local_kernel, out_shape=shapes, in_specs=[vm, vm, sm, vm,...  63 us
    pallas_call x1, Pallas kernels, comm_part(): pl.pallas_call(comm_kernel, out_shape=shapes, in_specs=[vm] * 5, out_spec...  36.6 us
    unnamed x17, local copies, waits for them, and re-layouts  6.79 us

profile of v4, /device:TPU:1, one launch (start us, length us, event | category | flops | bytes accessed | tf_op | source)
XLA Modules:
  0.0 110.3 jit_solution(4850070708885810052)
XLA Ops:
  0.6 0.0 copy-start.5
  1.3 0.0 copy-start.4
  2.0 0.0 copy-start.6
  2.0 0.0 copy-done.5
  2.0 0.0 copy-done.4
  2.0 0.7 copy-done.6
  2.7 0.0 copy-start
  2.7 1.0 copy-done
  3.7 0.0 copy-start.1
  3.7 1.0 copy-done.1
  4.7 0.0 copy-start.2
  4.7 1.0 copy-done.2
  5.7 0.0 copy-start.3
  5.7 0.9 copy-done.3
  6.6 63.0 %local_part.1 = (bf16[1024,256]{1,0:T(8,128)(2,1)}, bf16[1024,256]{1,0:T(8,128)(2,1)}, bf16[128,16,128]{2,1,0:T(8,128)(2,1)S(1)}, f32[2,1,128]{2,1,0:T(1,128)S(1)}, f32[2,16,256]{2,1,0:T(8,128)S(1)}) custom-call(bf16[1024,256]{1,0:T(8,128)(2,1)S(1)} %bitcast.10, s32[1,1024]{1,0:T(1,128)S(1)} %copy-done.5, s32[1,1]{1,0:T(1,128)S(6)} %copy.19.counts_ref, ...), custom_call_target="tpu_custom_call" | custom-call | tf_op jit(solution)/shard_map/local_part/pallas_call | solution.py:356
  69.6 0.7 fusion
  70.3 36.6 %comm_part.1 = (bf16[32,256]{1,0:T(8,128)(2,1)S(1)}, f32[256,768]{1,0:T(8,128)S(1)}, f32[256,256]{1,0:T(8,128)S(1)}, f32[1,256]{1,0:T(1,128)S(1)}) custom-call(bf16[128,16,128]{2,1,0:T(8,128)(2,1)S(1)} %get-tuple-element.39.send_ref, f32[2,1,128]{2,1,0:T(1,128)S(1)} %get-tuple-element.40.gsum_ref, f32[2,16,256]{2,1,0:T(8,128)S(1)} %get-tuple-element.41.edge_ref, ...), custom_call_target="tpu_custom_call" | custom-call | tf_op jit(solution)/shard_map/comm_part/pallas_call | solution.py:545
  106.9 0.6 bitcast_dynamic-update-slice_fusion.1
  107.5 0.6 bitcast_dynamic-update-slice_fusion
  108.1 0.9 copy.21
  109.0 0.7 copy.22
  109.7 0.6 copy.23
  (1 shorter events, 0.0 us)
Async XLA Ops:
  0.6 1.3 %copy-start.5 = (s32[1,1024]{1,0:T(1,128)S(1)}, s32[1,1024]{1,0:T(1,128)}, u32[]{:S(2)}) copy-start(s32[1,1024]{1,0:T(1,128)} %serial_ref.1) | copy-start | bytes 12292
  1.3 0.7 copy-start.4
  2.0 0.7 copy-start.6
  2.7 1.0 copy-start
  3.7 1.0 copy-start.1
  4.7 1.0 copy-start.2
  5.7 0.9 copy-start.3

commit v5 on v4

--- a/solution.py
+++ b/solution.py
@@ -66,6 +66,7 @@
     send_ref,
     gsum_ref,
     edge_ref,
+    rim_ref,
     gath_ref,
     hid_ref,
     normed_ref,
@@ -336,6 +337,8 @@
 
     lax.fori_loop(0, N // span, pool, 0)
     pooled_ref[...] = bo2_ref[...].astype(BF16)
+    rim_ref[:16, :] = bo2_ref[:16, :].astype(BF16)
+    rim_ref[16:, :] = bo2_ref[N - 16 :, :].astype(BF16)
     edge_ref[0, :8, :] = bo2_ref[:8, :]
     edge_ref[1, :8, :] = bo2_ref[N - 8 :, :]
     flag = jnp.full((8, C), joined_ref[0], jnp.int32).astype(F32)
@@ -350,6 +353,7 @@
         jax.ShapeDtypeStruct((128, 16, 128), BF16),
         jax.ShapeDtypeStruct((2, 1, 128), F32),
         jax.ShapeDtypeStruct((2, 16, C), F32),
+        jax.ShapeDtypeStruct((32, C), BF16),
     )
     vm = pl.BlockSpec(memory_space=VMEM)
     sm = pl.BlockSpec(memory_space=pltpu.SMEM)
@@ -357,7 +361,7 @@
         local_kernel,
         out_shape=shapes,
         in_specs=[vm, vm, sm, vm, vm, vm, vm, vm, sm],
-        out_specs=[vm] * 5,
+        out_specs=[vm] * 6,
         scratch_shapes=[
             VMEM((N, C), BF16),
             VMEM((N, C), BF16),
@@ -385,7 +389,7 @@
             VMEM((2, AQ, N), BF16),
             VMEM((2, AQ, N), BF16),
         ],
-        compiler_params=pltpu.CompilerParams(vmem_limit_bytes=46 * 1024 * 1024),
+        compiler_params=pltpu.CompilerParams(vmem_limit_bytes=56 * 1024 * 1024),
         name="local_part",
     )(raw, serial, counts, gain, w_qkv, w_proj, out_grad, cluster, joined)
 
@@ -562,17 +566,16 @@
             pltpu.SemaphoreType.DMA((18,)),
         ],
         compiler_params=pltpu.CompilerParams(
-            collective_id=0, has_side_effects=True, vmem_limit_bytes=16 * 1024 * 1024
+            collective_id=0, has_side_effects=True, vmem_limit_bytes=32 * 1024 * 1024
         ),
         name="comm_part",
     )(send, gsum, edge, ends, cluster)
 
 
 def body(raw_feats, serial, counts, norm_gain, w_qkv, w_proj, out_grad, cluster, joined):
-    pooled, grad_feats, send, gsum, edge = local_part(
+    pooled, grad_feats, send, gsum, edge, ends = local_part(
         raw_feats[0], serial, counts, norm_gain[None], w_qkv, w_proj, out_grad[0], cluster, joined
     )
-    ends = jnp.concatenate([pooled[:16], pooled[N - 16 :]], axis=0)
     ends, grad_qkv, grad_proj, grad_gain = comm_part(send, gsum, edge, ends, cluster)
     pooled = pooled.at[:16].set(ends[:16]).at[N - 16 :].set(ends[16:])
     return (pooled[None], grad_feats[None], grad_qkv, grad_proj, grad_gain[0])

time: 110 us -> 110 us (level)
  local copies, waits for them, and re-layouts: 8.7 us -> 6.55 us
  Pallas kernels: 99.5 us -> 101 us
    pallas_call x1, Pallas kernels: 63 us -> 70.5 us  [local_part(): pl.pallas_call(local_kernel, out_shape=shapes, in_specs=[vm, vm, sm, vm,...]
    pallas_call x1, Pallas kernels: 36.6 us -> 30.8 us  [comm_part(): pl.pallas_call(comm_kernel, out_shape=shapes, in_specs=[vm] * 5, out_spec...]
    unnamed x17 -> x13, local copies, waits for them, and re-layouts: 6.79 us -> 5.34 us
where the time goes in v5:
time: 110 us
  Pallas kernels  101 us (92%)
  local copies, waits for them, and re-layouts  6.55 us (6%)
  between operations  1.95 us (2%)
    pallas_call x1, Pallas kernels, local_part(): pl.pallas_call(local_kernel, out_shape=shapes, in_specs=[vm, vm, sm, vm,...  70.5 us
    pallas_call x1, Pallas kernels, comm_part(): pl.pallas_call(comm_kernel, out_shape=shapes, in_specs=[vm] * 5, out_spec...  30.8 us
    unnamed x13, local copies, waits for them, and re-layouts  5.34 us

profile of v5, /device:TPU:1, one launch (start us, length us, event | category | flops | bytes accessed | tf_op | source)
XLA Modules:
  0.0 109.8 jit_solution(3065565841781648721)
XLA Ops:
  1.9 70.5 %local_part.1 = (bf16[1024,256]{1,0:T(8,128)(2,1)}, bf16[1024,256]{1,0:T(8,128)(2,1)}, bf16[128,16,128]{2,1,0:T(8,128)(2,1)}, f32[2,1,128]{2,1,0:T(1,128)}, f32[...) custom-call(bf16[1024,256]{1,0:T(8,128)(2,1)} %bitcast.11, s32[1,1024]{1,0:T(1,128)} %serial_ref.1, ...), custom_call_target="tpu_custom_call" | custom-call | tf_op jit(solution)/shard_map/local_part/pallas_call | solution.py:360
  72.4 0.0 copy-start.2
  72.4 0.0 copy-start.4
  72.4 0.7 copy-done.2
  73.1 0.0 copy-done.4
  73.1 0.0 copy-start
  73.1 1.0 copy-done
  74.1 0.0 copy-start.1
  74.1 0.8 copy-done.1
  74.9 0.0 copy-start.3
  74.9 0.7 copy-done.3
  75.6 30.8 %comm_part.1 = (bf16[32,256]{1,0:T(8,128)(2,1)S(1)}, f32[256,768]{1,0:T(8,128)S(1)}, f32[256,256]{1,0:T(8,128)S(1)}, f32[1,256]{1,0:T(1,128)S(1)}) custom-call(bf16[128,16,128]{2,1,0:T(8,128)(2,1)S(1)} %copy-done, f32[2,1,128]{2,1,0:T(1,128)S(1)} %copy-done.4, f32[2,16,256]{2,1,0:T(8,128)S(1)} %copy-done.1, bf16[32,256]{1,0:T(8,128)(2,1)S(1)} %copy-done.3, ...), custom_call_target="tpu_custom_call" | custom-call | tf_op jit(solution)/shard_map/comm_part/pallas_call | solution.py:549
  106.4 0.6 bitcast_dynamic-update-slice_fusion.1
  107.0 0.6 bitcast_dynamic-update-slice_fusion
  107.6 0.9 copy.21
  108.5 0.7 copy.22
  109.2 0.6 copy.23
Async XLA Ops:
  72.4 0.7 copy-start.2
  72.4 0.7 copy-start.4
  73.1 1.0 copy-start
  74.1 0.8 copy-start.1
  74.9 0.7 copy-start.3

commit v6 on v3

--- a/solution.py
+++ b/solution.py
@@ -14,7 +14,7 @@
 HD = 16
 QB = 256
 NQ = N // QB
-AQ = 512
+AQ = 1024
 NA = N // AQ
 LAG = False
 GROUP = 8
@@ -328,15 +328,13 @@
     def pool(i, carry):
         at = pl.multiple_of(i * span, span)
         ids = ids_ref[pl.ds(at, wide), :]
+        shifts = (1, 2, 4, wide - 1, wide - 2, wide - 4)
+        same = [pltpu.roll(ids, step, 0) == ids for step in shifts]
         for half in range(2):
             cols = slice(half * 128, (half + 1) * 128)
             m = bo_ref[pl.ds(at, wide), cols]
-            for step in (1, 2, 4):
-                ok = pltpu.roll(ids, step, 0) == ids
+            for step, ok in zip(shifts, same):
                 m = jnp.maximum(m, jnp.where(ok, pltpu.roll(m, step, 0), -jnp.inf))
-            for step in (1, 2, 4):
-                ok = pltpu.roll(ids, wide - step, 0) == ids
-                m = jnp.maximum(m, jnp.where(ok, pltpu.roll(m, wide - step, 0), -jnp.inf))
             bo2_ref[pl.ds(at, span), cols] = m[8 : span + 8]
         return carry
 

time: 104 us -> 110 us (1.058); the launches traced: 102 us -> 110 us
  Pallas kernels: 94.2 us -> 102 us
    pallas_call x1, Pallas kernels: 65.1 us -> 70.3 us  [local_part(): pl.pallas_call(local_kernel, out_shape=shapes, in_specs=[vm, vm, sm, vm,...]
    pallas_call x1, Pallas kernels: 29.1 us -> 31.8 us  [comm_part(): pl.pallas_call(comm_kernel, out_shape=shapes, in_specs=[vm] * 5, out_spec...]
where the time goes in v6:
time: 110 us
  Pallas kernels  102 us (93%)
  local copies, waits for them, and re-layouts  5.8 us (5%)
  between operations  1.94 us (2%)
    pallas_call x1, Pallas kernels, local_part(): pl.pallas_call(local_kernel, out_shape=shapes, in_specs=[vm, vm, sm, vm,...  70.3 us
    pallas_call x1, Pallas kernels, comm_part(): pl.pallas_call(comm_kernel, out_shape=shapes, in_specs=[vm] * 5, out_spec...  31.8 us
    unnamed x11, local copies, waits for them, and re-layouts  3.88 us

profile of v6, /device:TPU:1, one launch (start us, length us, event | category | flops | bytes accessed | tf_op | source)
XLA Modules:
  0.0 109.9 jit_solution(15084746314448644820)
XLA Ops:
  1.9 70.3 %local_part.1 = (bf16[1024,256]{1,0:T(8,128)(2,1)}, bf16[1024,256]{1,0:T(8,128)(2,1)}, bf16[128,16,128]{2,1,0:T(8,128)(2,1)}, f32[2,1,128]{2,1,0:T(1,128)}, f32[2,16,256]{2,1,0:T(8,128)}) custom-call(bf16[1024,256]{1,0:T(8,128)(2,1)} %bitcast.11, s32[1,1024]{1,0:T(1,128)} %serial_ref.1, s32[1,1]{1,0:T(1,128)S(6)} %copy.19.counts_ref, f32[1,256]{1,0:T(1,128)} %bitcast.13, ...), custom_call_target="tpu_custom_call" | custom-call | tf_op jit(solution)/shard_map/local_part/pallas_call | solution.py:360
  72.2 0.0 copy-start.1
  72.2 0.7 fusion
  72.9 0.0 copy-start.2
  72.9 0.0 copy-start.3
  72.9 0.1 copy-done.1
  73.0 0.6 copy-done.2
  73.6 0.0 copy-done.3
  73.6 0.0 copy-start
  73.6 1.0 copy-done
  74.7 31.8 %comm_part.1 = (bf16[32,256]{1,0:T(8,128)(2,1)S(1)}, f32[256,768]{1,0:T(8,128)S(1)}, f32[256,256]{1,0:T(8,128)S(1)}, f32[1,256]{1,0:T(1,128)S(1)}) custom-call(bf16[128,16,128]{2,1,0:T(8,128)(2,1)S(1)} %copy-done, f32[2,1,128]{2,1,0:T(1,128)S(1)} %copy-done.3, f32[2,16,256]{2,1,0:T(8,128)S(1)} %copy-done.1, bf16[32,256]{1,0:T(8,128)(2,1)S(1)} %pad_maximum_fusion.ends_in_ref, ...), custom_call_target="tpu_custom_call" | custom-call | tf_op jit(solution)/shard_map/comm_part/pallas_call | solution.py:549
  106.5 0.6 bitcast_dynamic-update-slice_fusion.1
  107.1 0.6 bitcast_dynamic-update-slice_fusion
  107.7 0.9 copy.21
  108.6 0.7 copy.22
  109.3 0.6 copy.23
  (1 shorter events, 0.0 us)
Async XLA Ops:
  72.2 0.8 copy-start.1
  72.9 0.7 copy-start.2
  72.9 0.7 copy-start.3
  73.6 1.0 copy-start
